TPU v7x, 512 devices: a whole 4x8x8 slice. The times are simulated.
512 devices in a mesh: gx: 8 (over z), gy: 4 (over x), gz: 16 (over y, core).
Axes of the slice: x: 4, y: 8, z: 8, core: 2. Of those that a mesh axis runs over, the one named last changes fastest.
Arguments:
- velocity: float32 [3, 64, 32, 2048], P(None, 'gx', 'gy', 'gz'), may hold values from -6 to 6
- direction: float32 [3, 64, 32, 2048], P(None, 'gx', 'gy', 'gz'), may hold values from -3 to 3
- pressure: float32 [64, 32, 2048], P('gx', 'gy', 'gz'), may hold values from -6 to 6
- body_force: float32 [3, 64, 32, 2048], P(None, 'gx', 'gy', 'gz'), may hold values from -21 to 21, as said below
- phase_ids: int32 [64, 32, 2048], P('gx', 'gy', 'gz'), may hold values from 0 to 3
- creep_factor: float32 [4], replicated, may hold values from 0.5 to 2
- stress_exponent: float32 [4], replicated, may hold values from 1.5 to 4
- yield_stress: float32 [4], replicated, may hold values from 0.5 to 3
- accepted: int32 [1], replicated, may hold values from 0 to 3
Outputs:
- norms: float32 [2, 4], replicated
- chosen_velocity: float32 [3, 64, 32, 2048], P(None, 'gx', 'gy', 'gz')
- chosen_residual: float32 [3, 64, 32, 2048], P(None, 'gx', 'gy', 'gz')
Inputs may be any that keep to these rules, and one draw needn't show every extreme that they name: `body_force`: body force on every cell and component.
All inputs are finite; a program needn't handle non-finite values.
Results may differ from a plain program's by a relative error of at most 0.00022.
Values sent between devices are 32-bit elements; how exact they have to be, the bound alone decides.
A program may use at most 64 MiB of HBM per device.

v0:
```python
import jax
import jax.numpy as jnp
from jax import lax
from jax.sharding import Mesh
from jax.sharding import PartitionSpec as P

GX_GY_GZ = ("gx", "gy", "gz_0", "gz_1")
GZ = ("gz_0", "gz_1")


step_lengths = (1.0, 0.5, 0.25, 0.125)
rate_offset = 0.01
viscosity_least = 0.05
tiny_mean = 1e-06
tensor_slots = ((0, 3, 4), (3, 1, 5), (4, 5, 2))


def with_halo(array, sides, width):
    edges = {}
    for axis, dim in sides:
        size, length = (lax.axis_size(axis), array.shape[dim])
        up = [(i, (i + 1) % size) for i in range(size - 1)]
        last = lax.slice_in_dim(array, length - width, length, axis=dim)
        leading = lax.slice_in_dim(array, 0, width, axis=dim)
        edges[dim] = (
            lax.ppermute(last, axis, up),
            lax.ppermute(leading, axis, [(b, a) for a, b in up]),
        )
    done = []
    for _, dim in sides:
        low, high = edges[dim]
        around = [(width, width) if d in done else (0, 0) for d in range(array.ndim)]
        array = jnp.concatenate([jnp.pad(low, around), array, jnp.pad(high, around)], axis=dim)
        done.append(dim)
    return array


def extended(array, sides, width):
    for axis, dim in sides:
        size, length = (lax.axis_size(axis), array.shape[dim])
        up = [(i, (i + 1) % size) for i in range(size - 1)]
        down = [(j, i) for i, j in up]
        last = lax.slice_in_dim(array, length - width, length, axis=dim)
        leading = lax.slice_in_dim(array, 0, width, axis=dim)
        before = lax.ppermute(last, axis, up)
        after = lax.ppermute(leading, axis, down)
        array = jnp.concatenate([before, array, after], axis=dim)
    return array


def over_axes(array, axes):
    for axis in axes:
        array = lax.psum(array, axis)
    return array


def centered(values, axis_number):
    lower = [slice(1, -1)] * 3
    upper = [slice(1, -1)] * 3
    lower[axis_number] = slice(0, -2)
    upper[axis_number] = slice(2, None)
    leading = (slice(None),) * (values.ndim - 3)
    return 0.5 * (values[leading + tuple(upper)] - values[leading + tuple(lower)])


def component(values, i):
    return lax.index_in_dim(values, i, values.ndim - 4, keepdims=False)


def strain_rates(padded):
    gradients = [[centered(component(padded, i), j) for j in range(3)] for i in range(3)]
    return jnp.stack(
        [
            gradients[0][0],
            gradients[1][1],
            gradients[2][2],
            0.5 * (gradients[0][1] + gradients[1][0]),
            0.5 * (gradients[0][2] + gradients[2][0]),
            0.5 * (gradients[1][2] + gradients[2][1]),
        ],
        axis=-4,
    )


def double_dot(first, second):
    diagonal = (
        component(first, 0) * component(second, 0)
        + component(first, 1) * component(second, 1)
        + component(first, 2) * component(second, 2)
    )
    offdiag = (
        component(first, 3) * component(second, 3)
        + component(first, 4) * component(second, 4)
        + component(first, 5) * component(second, 5)
    )
    return diagonal + 2.0 * offdiag


def effective_viscosity(rates, factor, exponent, yields):
    second = 0.5 * double_dot(rates, rates) + rate_offset
    creep_part = factor * jnp.power(second, (1.0 - exponent) / (2.0 * exponent))
    plastic = 0.5 * yields * lax.rsqrt(second)
    total_part = creep_part + plastic
    viscosity = creep_part * plastic / total_part + viscosity_least
    creep_slope = creep_part * (1.0 - exponent) / (2.0 * exponent * second)
    plastic_slope = -plastic / (2.0 * second)
    derivative = (plastic * plastic * creep_slope + creep_part * creep_part * plastic_slope) / (
        total_part * total_part
    )
    return (viscosity, derivative)


def spread_cells(values):
    return jnp.expand_dims(values, values.ndim - 3)


def divergence(padded):
    return jnp.stack(
        [
            centered(component(padded, tensor_slots[i][0]), 0)
            + centered(component(padded, tensor_slots[i][1]), 1)
            + centered(component(padded, tensor_slots[i][2]), 2)
            for i in range(3)
        ],
        axis=-4,
    )


def tangent_stress(viscosity, derivative, rates, change):
    return (
        2.0 * spread_cells(viscosity) * change
        + 2.0 * spread_cells(derivative * double_dot(rates, change)) * rates
    )


def phase_params(phase_ids, creep_factor, stress_exponent, yield_stress):
    choose = (
        phase_ids[None] == jnp.arange(creep_factor.shape[0], dtype=jnp.int32)[:, None, None, None]
    ).astype(jnp.float32)
    return tuple(
        (
            jnp.sum(choose * entries[:, None, None, None], axis=0)
            for entries in (creep_factor, stress_exponent, yield_stress)
        )
    )


def edge_mask(start, count, devices):
    spots = start * count - 1 + jnp.arange(count + 2, dtype=jnp.int32)
    return ((spots >= 0) & (spots < count * devices)).astype(jnp.float32)


def stress_stack(base_rates, change_rates, trial_rates, factor, exponent, yields):
    base_viscosity, base_slope = effective_viscosity(base_rates, factor, exponent, yields)
    trial_viscosity, unused_slope = effective_viscosity(trial_rates, factor, exponent, yields)
    base_stress = 2.0 * spread_cells(base_viscosity) * base_rates
    change_stress = tangent_stress(base_viscosity, base_slope, base_rates, change_rates)
    trial_stress = 2.0 * spread_cells(trial_viscosity) * trial_rates
    return jnp.concatenate([base_stress[None], change_stress[None], trial_stress], axis=0)


def body(
    velocity,
    direction,
    pressure,
    body_force,
    phase_ids,
    creep_factor,
    stress_exponent,
    yield_stress,
    accepted,
):
    padded_pressure = with_halo(pressure, (("gx", 0), ("gy", 1), (GZ, 2)), 1)
    loading = body_force - jnp.stack([centered(padded_pressure, j) for j in range(3)])
    paired = extended(jnp.stack([velocity, direction]), (("gx", 2), ("gy", 3), (GZ, 4)), 2)
    phase_wide = extended(phase_ids, (("gx", 0), ("gy", 1), (GZ, 2)), 2)
    wide_factor, wide_exponent, wide_yields = phase_params(
        phase_wide[1:-1, 1:-1, 1:-1], creep_factor, stress_exponent, yield_stress
    )
    trial_padded = jnp.stack([paired[0] + length * paired[1] for length in step_lengths])
    stresses = stress_stack(
        strain_rates(paired[0]),
        strain_rates(paired[1]),
        strain_rates(trial_padded),
        wide_factor,
        wide_exponent,
        wide_yields,
    )
    mask_x = edge_mask(lax.axis_index("gx"), velocity.shape[1], lax.axis_size("gx"))
    mask_y = edge_mask(lax.axis_index("gy"), velocity.shape[2], lax.axis_size("gy"))
    mask_z = edge_mask(lax.axis_index(GZ), velocity.shape[3], lax.axis_size(GZ))
    padded_stress = stresses * (
        mask_x[:, None, None] * mask_y[None, :, None] * mask_z[None, None, :]
    )
    divided = divergence(padded_stress)
    residual_base = divided[0] + loading
    jacobian = divided[1]
    trial_residuals = divided[2:] + loading[None]
    actual = []
    predicted = []
    chosen_velocity = jnp.zeros_like(velocity)
    chosen_residual = jnp.zeros_like(velocity)
    for number, length in enumerate(step_lengths):
        trial_residual = trial_residuals[number]
        linear = residual_base + length * jacobian
        actual.append(jnp.sum(trial_residual * trial_residual))
        predicted.append(jnp.sum(linear * linear))
        picked = accepted[0] == number
        chosen_velocity = jnp.where(picked, velocity + length * direction, chosen_velocity)
        chosen_residual = jnp.where(picked, trial_residual, chosen_residual)
    sums = over_axes(jnp.stack(actual + predicted), GX_GY_GZ)
    cells = (
        3.0
        * velocity.shape[1]
        * velocity.shape[2]
        * velocity.shape[3]
        * lax.axis_size("gx")
        * lax.axis_size("gy")
        * lax.axis_size(GZ)
    )
    norms = jnp.sqrt(sums / cells + tiny_mean).reshape(2, 4)
    return (norms, chosen_velocity, chosen_residual)


def solution(mesh):
    torus = Mesh(
        mesh.devices.reshape(mesh.shape["gx"], mesh.shape["gy"], 8, 2), ("gx", "gy", "gz_0", "gz_1")
    )
    in_specs = (
        P(None, "gx", "gy", GZ),
        P(None, "gx", "gy", GZ),
        P("gx", "gy", GZ),
        P(None, "gx", "gy", GZ),
        P("gx", "gy", GZ),
        P(),
        P(),
        P(),
        P(),
    )
    out_specs = (P(), P(None, "gx", "gy", GZ), P(None, "gx", "gy", GZ))
    return jax.shard_map(body, mesh=torus, in_specs=in_specs, out_specs=out_specs, check_vma=False)
```

profile of v0, /device:TPU:1, one launch (start us, length us, event | category | flops | bytes accessed | tf_op | source)
XLA Modules:
  0.0 151.0 jit_solution(7799522047651627544)
XLA Ops:
  1.5 4.8 %collective-permute-start.6 = (f32[2,3,2,8,128]{4,3,2,1,0:T(8,128)S(1)}, f32[2,3,2,8,128]{4,3,2,1,0:T(8,128)S(1)}, u32[]{:S(2)}, u32[]{:S(2)}) collective-permute-start(f32[2,3,2,8,128]{4,3,2,1,0:T(8,128)S(1)} %get-tuple-element.60), channel_id=1, source_target_pairs={{0,64},{64,128},{128,192},{192,256},{256,320},{320,384},{384,448},... | collective-permute-start | bytes 147464 | tf_op jit(solution)/shard_map/ppermute | solution.py:45
  7.1 4.0 %collective-permute-start = (s32[2,8,128]{2,1,0:T(8,128)S(1)}, s32[2,8,128]{2,1,0:T(8,128)S(1)}, u32[]{:S(2)}, u32[]{:S(2)}) collective-permute-start(s32[2,8,128]{2,1,0:T(8,128)S(1)} %get-tuple-element.77), channel_id=1, source_target_pairs={{0,64},{64,128},{128,192},{192,256},{256,320},{320,384},{384,448},... | collective-permute-start | bytes 24584 | tf_op jit(solution)/shard_map/ppermute | solution.py:45
  13.1 4.6 %collective-permute-start.13 = (f32[1,8,128]{2,1,0:T(8,128)S(1)}, f32[1,8,128]{2,1,0:T(8,128)S(1)}, u32[]{:S(2)}, u32[]{:S(2)}) collective-permute-start(f32[1,8,128]{2,1,0:T(8,128)S(1)} %get-tuple-element.75), channel_id=1, source_target_pairs={{0,64},{64,128},{128,192},{192,256},{256,320},{320,384},{384,448},... | collective-permute-start | bytes 12296 | tf_op jit(solution)/shard_map/ppermute | solution.py:26
  23.9 3.1 %collective-permute-start.15 = (f32[8,1,128]{2,1,0:T(1,128)S(1)}, f32[8,1,128]{2,1,0:T(1,128)S(1)}, u32[]{:S(2)}, u32[]{:S(2)}) collective-permute-start(f32[8,1,128]{2,1,0:T(1,128)S(1)} %get-tuple-element.72), channel_id=1, source_target_pairs={{0,16},{16,32},{32,48},{1,17},{17,33},{33,49},{2,18},{18,34},{34,5... | collective-permute-start | bytes 12296 | tf_op jit(solution)/shard_map/ppermute | solution.py:26
  28.7 3.1 %collective-permute-start.2 = (s32[12,2,128]{2,1,0:T(2,128)S(1)}, s32[12,2,128]{2,1,0:T(2,128)S(1)}, u32[]{:S(2)}, u32[]{:S(2)}) collective-permute-start(s32[12,2,128]{2,1,0:T(2,128)S(1)} %get-tuple-element.66), channel_id=1, source_target_pairs={{0,16},{16,32},{32,48},{1,17},{17,33},{33,49},{2,18},{18,34},{34,5... | collective-permute-start | bytes 36872 | tf_op jit(solution)/shard_map/ppermute | solution.py:45
  34.5 4.9 %collective-permute-start.16 = (f32[8,8,1]{2,1,0:T(8,128)S(1)}, f32[8,8,1]{2,1,0:T(8,128)S(1)}, u32[]{:S(2)}, u32[]{:S(2)}) collective-permute-start(f32[8,8,1]{2,1,0:T(8,128)S(1)} %get-tuple-element.70), channel_id=1, source_target_pairs={{1,0},{2,1},{3,2},{4,3},{5,4},{6,5},{7,6},{8,7},{9,8},{10,9},{11,1... | collective-permute-start | bytes 776 | tf_op jit(solution)/shard_map/ppermute | solution.py:27
  39.3 3.1 %collective-permute-start.17 = (f32[8,8,1]{2,1,0:T(8,128)S(1)}, f32[8,8,1]{2,1,0:T(8,128)S(1)}, u32[]{:S(2)}, u32[]{:S(2)}) collective-permute-start(f32[8,8,1]{2,1,0:T(8,128)S(1)} %get-tuple-element.71), channel_id=1, source_target_pairs={{0,1},{1,2},{2,3},{3,4},{4,5},{5,6},{6,7},{7,8},{8,9},{9,10},{10,1... | collective-permute-start | bytes 776 | tf_op jit(solution)/shard_map/ppermute | solution.py:26
  42.6 2.4 %collective-permute-start.4 = (s32[12,12,2]{2,1,0:T(8,128)S(1)}, s32[12,12,2]{2,1,0:T(8,128)S(1)}, u32[]{:S(2)}, u32[]{:S(2)}) collective-permute-start(s32[12,12,2]{2,1,0:T(8,128)S(1)} %get-tuple-element.62), channel_id=1, source_target_pairs={{0,1},{1,2},{2,3},{3,4},{4,5},{5,6},{6,7},{7,8},{8,9},{9,10},{10,1... | collective-permute-start | bytes 3464 | tf_op jit(solution)/shard_map/ppermute | solution.py:45
  45.0 1.9 %collective-permute-start.5 = (s32[12,12,2]{2,1,0:T(8,128)S(1)}, s32[12,12,2]{2,1,0:T(8,128)S(1)}, u32[]{:S(2)}, u32[]{:S(2)}) collective-permute-start(s32[12,12,2]{2,1,0:T(8,128)S(1)} %get-tuple-element.63), channel_id=1, source_target_pairs={{1,0},{2,1},{3,2},{4,3},{5,4},{6,5},{7,6},{8,7},{9,8},{10,9},{11,1... | collective-permute-start | bytes 3464 | tf_op jit(solution)/shard_map/ppermute | solution.py:46
  47.1 3.9 %collective-permute-done.5 = s32[12,12,2]{2,1,0:T(8,128)S(1)} collective-permute-done((s32[12,12,2]{2,1,0:T(8,128)S(1)}, s32[12,12,2]{2,1,0:T(8,128)S(1)}, u32[]{:S(2)}, u32[]{:S(2)}) %collective-permute-start.5) | collective-permute-done | bytes 1184 | tf_op jit(solution)/shard_map/ppermute | solution.py:46
  52.3 4.3 %collective-permute-start.8 = (f32[2,3,12,2,128]{4,3,2,1,0:T(2,128)S(1)}, f32[2,3,12,2,128]{4,3,2,1,0:T(2,128)S(1)}, u32[]{:S(2)}, u32[]{:S(2)}) collective-permute-start(f32[2,3,12,2,128]{4,3,2,1,0:T(2,128)S(1)} %get-tuple-element.58), channel_id=1, source_target_pairs={{0,16},{16,32},{32,48},{1,17},{17,33},{33,49},{2,18},{18,34},{34,5... | collective-permute-start | bytes 221192 | tf_op jit(solution)/shard_map/ppermute | solution.py:45
  58.8 2.9 %collective-permute-done.9 = f32[2,3,12,2,128]{4,3,2,1,0:T(2,128)S(1)} collective-permute-done((f32[2,3,12,2,128]{4,3,2,1,0:T(2,128)S(1)}, f32[2,3,12,2,128]{4,3,2,1,0:T(2,128)S(1)}, u32[]{:S(2)}, u32[]{:S(2)}) %collective-permute-start.9) | collective-permute-done | bytes 73760 | tf_op jit(solution)/shard_map/ppermute | solution.py:46
  62.5 3.5 %collective-permute-start.10 = (f32[2,3,12,12,2]{3,4,2,1,0:T(2,128)S(1)}, f32[2,3,12,12,2]{3,4,2,1,0:T(2,128)S(1)}, u32[]{:S(2)}, u32[]{:S(2)}) collective-permute-start(f32[2,3,12,12,2]{3,4,2,1,0:T(2,128)S(1)} %copy.142), channel_id=1, source_target_pairs={{0,1},{1,2},{2,3},{3,4},{4,5},{5,6},{6,7},{7,8},{8,9},{9,10},{10,1... | collective-permute-start | bytes 20744 | tf_op jit(solution)/shard_map/ppermute | solution.py:45
  66.6 2.1 %collective-permute-start.11 = (f32[2,3,12,12,2]{3,4,2,1,0:T(2,128)S(1)}, f32[2,3,12,12,2]{3,4,2,1,0:T(2,128)S(1)}, u32[]{:S(2)}, u32[]{:S(2)}) collective-permute-start(f32[2,3,12,12,2]{3,4,2,1,0:T(2,128)S(1)} %copy.143), channel_id=1, source_target_pairs={{1,0},{2,1},{3,2},{4,3},{5,4},{6,5},{7,6},{8,7},{9,8},{10,9},{11,1... | collective-permute-start | bytes 20744 | tf_op jit(solution)/shard_map/ppermute | solution.py:46
  69.3 3.0 %collective-permute-done.11 = f32[2,3,12,12,2]{3,4,2,1,0:T(2,128)S(1)} collective-permute-done((f32[2,3,12,12,2]{3,4,2,1,0:T(2,128)S(1)}, f32[2,3,12,12,2]{3,4,2,1,0:T(2,128)S(1)}, u32[]{:S(2)}, u32[]{:S(2)}) %collective-permute-start.11) | collective-permute-done | bytes 6944 | tf_op jit(solution)/shard_map/ppermute | solution.py:46
  77.6 1.8 %pad_maximum_fusion = f32[4,3,12,12,132]{4,0,3,2,1:T(4,128)S(1)} fusion(f32[1,3,12,12,132]{4,0,3,2,1:T(1,128)S(1)} %copy.161, f32[1,3,12,12,132]{4,0,3,2,1:T(1,128)S(1)} %copy.160, f32[1,3,12,12,132]{4,0,3,2,1:T(1,128)S(1)} %copy.159, f32[1,3,12,12,132]{4,0,3,2,1:T(1,128)S(1)} %copy.158), kind=kLoop, calls=%fused_computation.1 | loop fusion | flops 684288 | bytes 1824768 | tf_op jit(solution)/shard_map/stack | solution.py:180
  83.4 3.7 %add_multiply_fusion = (f32[4,10,10,130]{3,0,2,1:T(4,128)S(1)}, f32[4,10,10,130]{3,0,2,1:T(4,128)S(1)}, f32[4,10,10,130]{3,0,2,1:T(4,128)S(1)}, f32[4,10,10,130]{3,0,2,1:T(4,128)S(1)}) fusion(f32[10,10,130]{2,1,0:T(8,128)S(1)} %get-tuple-element.79, f32[10,10,130]{2,1,0:T(8,128)S(1)} %get-tuple-element.78, f32[10,10,130]{2,1,0:T(8,128)S(1)} %get-tuple-element.14, ...), kind=kLoop, calls=%fused_computation.43 | loop fusion | flops 2028000 | bytes 4732000 | tf_op jit(solution)/shard_map/mul | solution.py:158
  88.5 1.9 %maximum_multiply_fusion = f32[6,6,10,10,130]{4,0,3,2,1:T(8,128)S(1)} fusion(f32[4,6,10,10,130]{4,0,3,2,1:T(4,128)S(1)} %bitcast.105, f32[1,6,10,10,130]{4,0,3,2,1:T(1,128)S(1)} %get-tuple-element.54, f32[1,6,10,10,130]{4,0,3,2,1:T(1,128)S(1)} %get-tuple-element.53, f32[10,10,130]{2,1,0:T(8,128)S(1)} %broadcast_multiply_fusion.2), kind=kLoop, calls=%fused_computation | loop fusion | flops 1404000 | bytes 3796000 | tf_op jit(solution)/shard_map/mul | solution.py:192
  93.0 1.3 multiply_reduce_fusion.4
  94.3 5.0 %stack.171 = f32[8]{0:T(128)S(1)} concatenate(f32[1]{0:T(128)} %bitcast.41, f32[1]{0:T(128)} %bitcast.42, f32[1]{0:T(128)} %bitcast.43, f32[1]{0:T(128)} %bitcast.44, f32[1]{0:T(128)} %bitcast.47, f32[1]{0:T(128)} %bitcast.48, f32[1]{0:T(128)} %bitcast.49, f32[1]{0:T(128)} %bitcast.50), dimensions={0} | concatenate | bytes 64 | tf_op jit(solution)/shard_map/stack | solution.py:211
  99.3 19.3 %psum.28 = f32[8]{0:T(128)S(1)} all-reduce(f32[8]{0:T(128)S(1)} %stack.171), channel_id=1, replica_groups=mesh['gx'=8,'gy'=4,'gz_0'=8,'gz_1'=2] {'gx'}, use_global_device_ids=true, to_apply=%region_11.12 | all-reduce | flops 8 | bytes 64 | tf_op jit(solution)/shard_map/psum | solution.py:53
  118.6 7.2 %psum.29 = f32[8]{0:T(128)S(1)} all-reduce(f32[8]{0:T(128)S(1)} %psum.28), channel_id=1, replica_groups=mesh['gx'=8,'gy'=4,'gz_0'=8,'gz_1'=2] {'gy'}, use_global_device_ids=true, to_apply=%region_12.13 | all-reduce | flops 8 | bytes 64 | tf_op jit(solution)/shard_map/psum | solution.py:53
  125.8 15.4 %psum.30 = f32[8]{0:T(128)S(1)} all-reduce(f32[8]{0:T(128)S(1)} %psum.29), channel_id=1, replica_groups=mesh['gx'=8,'gy'=4,'gz_0'=8,'gz_1'=2] {'gz_0'}, use_global_device_ids=true, to_apply=%region_13.14 | all-reduce | flops 8 | bytes 64 | tf_op jit(solution)/shard_map/psum | solution.py:53
  141.8 8.5 %psum.31 = f32[8]{0:T(128)S(1)} all-reduce(f32[8]{0:T(128)S(1)} %psum.30), channel_id=1, replica_groups=mesh['gx'=8,'gy'=4,'gz_0'=8,'gz_1'=2] {'gz_1'}, use_global_device_ids=true, to_apply=%region_14.15 | all-reduce | flops 8 | bytes 64 | tf_op jit(solution)/shard_map/psum | solution.py:53
  (108 shorter events, 33.4 us)
Async XLA Ops:
  0.6 61.0 %copy-start.1 = (f32[3,8,8,128]{3,2,1,0:T(8,128)S(1)}, f32[3,8,8,128]{3,2,1,0:T(8,128)}, u32[]{:S(2)}) copy-start(f32[3,8,8,128]{3,2,1,0:T(8,128)} %param.9) | copy-start | bytes 294916
  0.6 61.0 %copy-start = (f32[3,8,8,128]{3,2,1,0:T(8,128)S(1)}, f32[3,8,8,128]{3,2,1,0:T(8,128)}, u32[]{:S(2)}) copy-start(f32[3,8,8,128]{3,2,1,0:T(8,128)} %param.10) | copy-start | bytes 294916
  0.7 57.2 %copy-start.3 = (f32[4]{0:T(128)S(1)}, f32[4]{0:T(128)}, u32[]{:S(2)}) copy-start(f32[4]{0:T(128)} %param.14) | copy-start | bytes 52
  0.7 57.2 %copy-start.5 = (f32[4]{0:T(128)S(1)}, f32[4]{0:T(128)}, u32[]{:S(2)}) copy-start(f32[4]{0:T(128)} %param.15) | copy-start | bytes 52
  0.7 57.2 %copy-start.4 = (f32[4]{0:T(128)S(1)}, f32[4]{0:T(128)}, u32[]{:S(2)}) copy-start(f32[4]{0:T(128)} %param.16) | copy-start | bytes 52
  1.5 49.6 %collective-permute-start.6 = (f32[2,3,2,8,128]{4,3,2,1,0:T(8,128)S(1)}, f32[2,3,2,8,128]{4,3,2,1,0:T(8,128)S(1)}, u32[]{:S(2)}, u32[]{:S(2)}) collective-permute-start(f32[2,3,2,8,128]{4,3,2,1,0:T(8,128)S(1)} %get-tuple-element.60), channel_id=1, source_target_pairs={{0,64},{64,128},{128,192},{192,256},{256,320},{320,384},{384,448},... | collective-permute-start | bytes 147464 | tf_op jit(solution)/shard_map/ppermute | solution.py:45
  7.1 20.8 %collective-permute-start = (s32[2,8,128]{2,1,0:T(8,128)S(1)}, s32[2,8,128]{2,1,0:T(8,128)S(1)}, u32[]{:S(2)}, u32[]{:S(2)}) collective-permute-start(s32[2,8,128]{2,1,0:T(8,128)S(1)} %get-tuple-element.77), channel_id=1, source_target_pairs={{0,64},{64,128},{128,192},{192,256},{256,320},{320,384},{384,448},... | collective-permute-start | bytes 24584 | tf_op jit(solution)/shard_map/ppermute | solution.py:45
  11.1 17.6 %collective-permute-start.1 = (s32[2,8,128]{2,1,0:T(8,128)S(1)}, s32[2,8,128]{2,1,0:T(8,128)S(1)}, u32[]{:S(2)}, u32[]{:S(2)}) collective-permute-start(s32[2,8,128]{2,1,0:T(8,128)S(1)} %get-tuple-element.76), channel_id=1, source_target_pairs={{64,0},{128,64},{192,128},{256,192},{320,256},{384,320},{448,384},... | collective-permute-start | bytes 24584 | tf_op jit(solution)/shard_map/ppermute | solution.py:46
  13.1 8.5 %collective-permute-start.13 = (f32[1,8,128]{2,1,0:T(8,128)S(1)}, f32[1,8,128]{2,1,0:T(8,128)S(1)}, u32[]{:S(2)}, u32[]{:S(2)}) collective-permute-start(f32[1,8,128]{2,1,0:T(8,128)S(1)} %get-tuple-element.75), channel_id=1, source_target_pairs={{0,64},{64,128},{128,192},{192,256},{256,320},{320,384},{384,448},... | collective-permute-start | bytes 12296 | tf_op jit(solution)/shard_map/ppermute | solution.py:26
  17.7 6.2 %collective-permute-start.12 = (f32[1,8,128]{2,1,0:T(8,128)S(1)}, f32[1,8,128]{2,1,0:T(8,128)S(1)}, u32[]{:S(2)}, u32[]{:S(2)}) collective-permute-start(f32[1,8,128]{2,1,0:T(8,128)S(1)} %get-tuple-element.74), channel_id=1, source_target_pairs={{64,0},{128,64},{192,128},{256,192},{320,256},{384,320},{448,384},... | collective-permute-start | bytes 12296 | tf_op jit(solution)/shard_map/ppermute | solution.py:27
  21.6 11.5 %collective-permute-start.14 = (f32[8,1,128]{2,1,0:T(1,128)S(1)}, f32[8,1,128]{2,1,0:T(1,128)S(1)}, u32[]{:S(2)}, u32[]{:S(2)}) collective-permute-start(f32[8,1,128]{2,1,0:T(1,128)S(1)} %get-tuple-element.73), channel_id=1, source_target_pairs={{16,0},{32,16},{48,32},{17,1},{33,17},{49,33},{18,2},{34,18},{50,3... | collective-permute-start | bytes 12296 | tf_op jit(solution)/shard_map/ppermute | solution.py:27
  23.9 10.6 %collective-permute-start.15 = (f32[8,1,128]{2,1,0:T(1,128)S(1)}, f32[8,1,128]{2,1,0:T(1,128)S(1)}, u32[]{:S(2)}, u32[]{:S(2)}) collective-permute-start(f32[8,1,128]{2,1,0:T(1,128)S(1)} %get-tuple-element.72), channel_id=1, source_target_pairs={{0,16},{16,32},{32,48},{1,17},{17,33},{33,49},{2,18},{18,34},{34,5... | collective-permute-start | bytes 12296 | tf_op jit(solution)/shard_map/ppermute | solution.py:26
  28.7 10.7 %collective-permute-start.2 = (s32[12,2,128]{2,1,0:T(2,128)S(1)}, s32[12,2,128]{2,1,0:T(2,128)S(1)}, u32[]{:S(2)}, u32[]{:S(2)}) collective-permute-start(s32[12,2,128]{2,1,0:T(2,128)S(1)} %get-tuple-element.66), channel_id=1, source_target_pairs={{0,16},{16,32},{32,48},{1,17},{17,33},{33,49},{2,18},{18,34},{34,5... | collective-permute-start | bytes 36872 | tf_op jit(solution)/shard_map/ppermute | solution.py:45
  31.8 10.6 %collective-permute-start.3 = (s32[12,2,128]{2,1,0:T(2,128)S(1)}, s32[12,2,128]{2,1,0:T(2,128)S(1)}, u32[]{:S(2)}, u32[]{:S(2)}) collective-permute-start(s32[12,2,128]{2,1,0:T(2,128)S(1)} %get-tuple-element.67), channel_id=1, source_target_pairs={{16,0},{32,16},{48,32},{17,1},{33,17},{49,33},{18,2},{34,18},{50,3... | collective-permute-start | bytes 36872 | tf_op jit(solution)/shard_map/ppermute | solution.py:46
  33.1 18.0 %collective-permute-start.7 = (f32[2,3,2,8,128]{4,3,2,1,0:T(8,128)S(1)}, f32[2,3,2,8,128]{4,3,2,1,0:T(8,128)S(1)}, u32[]{:S(2)}, u32[]{:S(2)}) collective-permute-start(f32[2,3,2,8,128]{4,3,2,1,0:T(8,128)S(1)} %get-tuple-element.61), channel_id=1, source_target_pairs={{64,0},{128,64},{192,128},{256,192},{320,256},{384,320},{448,384},... | collective-permute-start | bytes 147464 | tf_op jit(solution)/shard_map/ppermute | solution.py:46
  34.5 10.5 %collective-permute-start.16 = (f32[8,8,1]{2,1,0:T(8,128)S(1)}, f32[8,8,1]{2,1,0:T(8,128)S(1)}, u32[]{:S(2)}, u32[]{:S(2)}) collective-permute-start(f32[8,8,1]{2,1,0:T(8,128)S(1)} %get-tuple-element.70), channel_id=1, source_target_pairs={{1,0},{2,1},{3,2},{4,3},{5,4},{6,5},{7,6},{8,7},{9,8},{10,9},{11,1... | collective-permute-start | bytes 776 | tf_op jit(solution)/shard_map/ppermute | solution.py:27
  39.3 7.6 %collective-permute-start.17 = (f32[8,8,1]{2,1,0:T(8,128)S(1)}, f32[8,8,1]{2,1,0:T(8,128)S(1)}, u32[]{:S(2)}, u32[]{:S(2)}) collective-permute-start(f32[8,8,1]{2,1,0:T(8,128)S(1)} %get-tuple-element.71), channel_id=1, source_target_pairs={{0,1},{1,2},{2,3},{3,4},{4,5},{5,6},{6,7},{7,8},{8,9},{9,10},{10,1... | collective-permute-start | bytes 776 | tf_op jit(solution)/shard_map/ppermute | solution.py:26
  42.6 4.5 %collective-permute-start.4 = (s32[12,12,2]{2,1,0:T(8,128)S(1)}, s32[12,12,2]{2,1,0:T(8,128)S(1)}, u32[]{:S(2)}, u32[]{:S(2)}) collective-permute-start(s32[12,12,2]{2,1,0:T(8,128)S(1)} %get-tuple-element.62), channel_id=1, source_target_pairs={{0,1},{1,2},{2,3},{3,4},{4,5},{5,6},{6,7},{7,8},{8,9},{9,10},{10,1... | collective-permute-start | bytes 3464 | tf_op jit(solution)/shard_map/ppermute | solution.py:45
  45.0 5.9 %collective-permute-start.5 = (s32[12,12,2]{2,1,0:T(8,128)S(1)}, s32[12,12,2]{2,1,0:T(8,128)S(1)}, u32[]{:S(2)}, u32[]{:S(2)}) collective-permute-start(s32[12,12,2]{2,1,0:T(8,128)S(1)} %get-tuple-element.63), channel_id=1, source_target_pairs={{1,0},{2,1},{3,2},{4,3},{5,4},{6,5},{7,6},{8,7},{9,8},{10,9},{11,1... | collective-permute-start | bytes 3464 | tf_op jit(solution)/shard_map/ppermute | solution.py:46
  52.3 6.5 %collective-permute-start.8 = (f32[2,3,12,2,128]{4,3,2,1,0:T(2,128)S(1)}, f32[2,3,12,2,128]{4,3,2,1,0:T(2,128)S(1)}, u32[]{:S(2)}, u32[]{:S(2)}) collective-permute-start(f32[2,3,12,2,128]{4,3,2,1,0:T(2,128)S(1)} %get-tuple-element.58), channel_id=1, source_target_pairs={{0,16},{16,32},{32,48},{1,17},{17,33},{33,49},{2,18},{18,34},{34,5... | collective-permute-start | bytes 221192 | tf_op jit(solution)/shard_map/ppermute | solution.py:45
  56.5 5.1 %collective-permute-start.9 = (f32[2,3,12,2,128]{4,3,2,1,0:T(2,128)S(1)}, f32[2,3,12,2,128]{4,3,2,1,0:T(2,128)S(1)}, u32[]{:S(2)}, u32[]{:S(2)}) collective-permute-start(f32[2,3,12,2,128]{4,3,2,1,0:T(2,128)S(1)} %get-tuple-element.59), channel_id=1, source_target_pairs={{16,0},{32,16},{48,32},{17,1},{33,17},{49,33},{18,2},{34,18},{50,3... | collective-permute-start | bytes 221192 | tf_op jit(solution)/shard_map/ppermute | solution.py:46
  62.5 6.2 %collective-permute-start.10 = (f32[2,3,12,12,2]{3,4,2,1,0:T(2,128)S(1)}, f32[2,3,12,12,2]{3,4,2,1,0:T(2,128)S(1)}, u32[]{:S(2)}, u32[]{:S(2)}) collective-permute-start(f32[2,3,12,12,2]{3,4,2,1,0:T(2,128)S(1)} %copy.142), channel_id=1, source_target_pairs={{0,1},{1,2},{2,3},{3,4},{4,5},{5,6},{6,7},{7,8},{8,9},{9,10},{10,1... | collective-permute-start | bytes 20744 | tf_op jit(solution)/shard_map/ppermute | solution.py:45
  66.6 5.7 %collective-permute-start.11 = (f32[2,3,12,12,2]{3,4,2,1,0:T(2,128)S(1)}, f32[2,3,12,12,2]{3,4,2,1,0:T(2,128)S(1)}, u32[]{:S(2)}, u32[]{:S(2)}) collective-permute-start(f32[2,3,12,12,2]{3,4,2,1,0:T(2,128)S(1)} %copy.143), channel_id=1, source_target_pairs={{1,0},{2,1},{3,2},{4,3},{5,4},{6,5},{7,6},{8,7},{9,8},{10,9},{11,1... | collective-permute-start | bytes 20744 | tf_op jit(solution)/shard_map/ppermute | solution.py:46
  90.9 1.2 copy-start.2
where the time goes:
time: 152 us; the launch traced here: 151 us
  blocking collectives  50.4 us (33%)
  starting transfers between devices  49.5 us (33%)
  other arithmetic  21.8 us (14%)
  local copies, waits for them, and re-layouts  16.6 us (11%)
  waiting for transfers between devices  10.7 us (7%)
  between operations  1.94 us (1%)
    psum x4, blocking collectives, over_axes(): array = lax.psum(array, axis)  50.4 us
    ppermute x6, starting transfers between devices, extended(): before = lax.ppermute(last, axis, up)  22.1 us
    ppermute x3, starting transfers between devices, with_halo(): lax.ppermute(last, axis, up)  10.8 us
    ppermute x6, waiting for transfers between devices, extended(): after = lax.ppermute(leading, axis, down)  9.7 us
    ppermute x6, starting transfers between devices, extended(): after = lax.ppermute(leading, axis, down)  9.18 us
    ppermute x3, starting transfers between devices, with_halo(): lax.ppermute(leading, axis, [(b, a) for a, b in up])  7.44 us
    another operation x1, local copies, waits for them, and re-layouts, body(): sums = over_axes(jnp.stack(actual + predicted), GX_GY_GZ)  4.97 us
    mul x2, other arithmetic, stress_stack(): trial_stress = 2.0 * spread_cells(trial_viscosity) * trial_rates  3.93 us
  transfers between devices with their start and end apart: 18, of which 4 were waited for; matrix products, arithmetic and copies ran while one was open for 5% of the time, Pallas kernels for 0%

commit v1 on v0

v1 whole, which is shorter than its diff:
```python
import functools

import jax
import jax.numpy as jnp
from jax import lax
from jax.experimental import pallas as pl
from jax.experimental.pallas import tpu as pltpu
from jax.sharding import PartitionSpec as P

MESH = pl.DeviceIdType.MESH
LENGTHS = (1.0, 0.5, 0.25, 0.125)
ROWS = 24
TOP = 8
ALONG = ((0, 3, 4), (3, 1, 5), (4, 5, 2))


def roll(values, shift, axis):
    return pltpu.roll(values, shift % values.shape[axis], axis)


def kernel(
    sizes,
    v_hbm, d_hbm, p_hbm, b_hbm, ph_hbm, fac_ref, exp_ref, yld_ref, acc_ref,
    norms_ref, cv_hbm, cr_hbm,
    VP, PP, HP, BF, YS, YR, WS, ZR, XZ, YZ, ES, ER, SS, CV, CR, RZ, RX, RY,
    load_sem, out_sem, send_sem, recv_sem, rz_sem, rx_sem, ry_sem,
):
    n = dict(zip(("gx", "gy", "gz"), sizes))
    me = {a: lax.axis_index(a) for a in n}
    has = {}
    for a in n:
        has[a, 1] = me[a] < n[a] - 1
        has[a, -1] = me[a] > 0
    f32 = jnp.float32
    lane = lax.broadcasted_iota(jnp.int32, (8, 128), 1)
    sub = lax.broadcasted_iota(jnp.int32, (8, 128), 0)
    odd = (lane & 1) == 1
    first_lane, last_lane = lane == 0, lane == 127

    block = pl.ds(TOP, 8)
    loads = [
        pltpu.make_async_copy(v_hbm, VP.at[pl.ds(0, 3), pl.ds(2, 8), block], load_sem.at[0]),
        pltpu.make_async_copy(d_hbm, VP.at[pl.ds(3, 3), pl.ds(2, 8), block], load_sem.at[1]),
        pltpu.make_async_copy(p_hbm, PP.at[pl.ds(1, 8), block], load_sem.at[2]),
        pltpu.make_async_copy(ph_hbm, HP.at[pl.ds(1, 8)], load_sem.at[3]),
        pltpu.make_async_copy(b_hbm, BF, load_sem.at[4]),
    ]
    for load in loads:
        load.start()

    zero = jnp.zeros((8, 128), f32)
    for c in range(6):
        for x in (0, 1, 10, 11):
            VP[c, x, block] = zero
    for x in (0, 9):
        PP[x, block] = zero
        HP[x] = jnp.zeros((8, 128), jnp.int32)
    for ref in (YR, ZR, XZ, YZ, ER):
        ref[...] = jnp.zeros(ref.shape, f32)

    counter = [0]

    def message(step, pairs):
        send = functools.reduce(jnp.logical_and, [has[a, s] for a, s in step.items()])
        recv = functools.reduce(jnp.logical_and, [has[a, -s] for a, s in step.items()])
        target = {a: me[a] + s for a, s in step.items()}
        copies = []
        for src, dst in pairs:
            i = counter[0]
            counter[0] += 1
            copies.append(
                pltpu.make_async_remote_copy(
                    src_ref=src, dst_ref=dst, send_sem=send_sem.at[i], recv_sem=recv_sem.at[i],
                    device_id=target, device_id_type=MESH,
                )
            )
        return send, recv, copies

    def start(messages):
        for send, _, copies in messages:
            @pl.when(send)
            def _():
                for copy in copies:
                    copy.start()

    def arrived(messages):
        for _, recv, copies in messages:
            @pl.when(recv)
            def _():
                for copy in copies:
                    copy.wait_recv()

    def sent(messages):
        for send, _, copies in messages:
            @pl.when(send)
            def _():
                for copy in copies:
                    copy.wait_send()

    both = (1, -1)
    hi = lambda s: (s + 1) // 2
    lo = lambda s: (1 - s) // 2
    x_near, x_far, y_near, y_far, z_face, xz_edge, yz_edge, xy_edge = ([] for _ in range(8))
    for s in both:
        near_from, near_to = (9, 1) if s == 1 else (2, 10)
        far_from, far_to = (8, 0) if s == 1 else (3, 11)
        p_from, p_to = (8, 0) if s == 1 else (1, 9)
        x_near.append(message({"gx": s}, [
            (VP.at[:, near_from, block], VP.at[:, near_to, block]),
            (PP.at[p_from, block], PP.at[p_to, block]),
        ]))
        x_far.append(message({"gx": s}, [
            (VP.at[:, far_from, block], VP.at[:, far_to, block]),
            (HP.at[p_from], HP.at[p_to]),
        ]))
        y_near.append(message({"gy": s}, [(YS.at[hi(s), pl.ds(0, 7)], YR.at[lo(s), pl.ds(0, 7)])]))
        y_far.append(message({"gy": s}, [(YS.at[hi(s), pl.ds(7, 7)], YR.at[lo(s), pl.ds(7, 7)])]))
        z_face.append(message({"gz": s}, [(WS.at[pl.ds(0, 2)], ZR.at[lo(s)])]))
        for t in both:
            xz_edge.append(message({"gx": s, "gz": t}, [(WS.at[pl.ds(1, 1)], XZ.at[lo(s), lo(t)])]))
            yz_edge.append(message({"gy": s, "gz": t}, [(WS.at[pl.ds(1, 2)], YZ.at[lo(s), lo(t)])]))
            xy_edge.append(message({"gx": s, "gy": t}, [(ES.at[hi(s), hi(t)], ER.at[lo(s), lo(t)])]))

    barrier = pltpu.get_barrier_semaphore()
    for a in n:
        for k in range(1, n[a]):
            pl.semaphore_signal(barrier, inc=1, device_id={a: lax.rem(me[a] + k, n[a])}, device_id_type=MESH)
    for a, b in (("gx", "gy"), ("gx", "gz"), ("gy", "gz")):
        for s in both:
            for t in both:
                @pl.when(jnp.logical_and(has[a, s], has[b, t]))
                def _():
                    pl.semaphore_signal(
                        barrier, inc=1, device_id={a: me[a] + s, b: me[b] + t}, device_id_type=MESH
                    )
    sides = {a: has[a, 1].astype(jnp.int32) + has[a, -1].astype(jnp.int32) for a in n}
    edges = sides["gx"] * sides["gy"] + sides["gx"] * sides["gz"] + sides["gy"] * sides["gz"]

    for load in loads[:4]:
        load.wait()

    def y_layer(c, y):
        return VP[c, pl.ds(2, 8), TOP + y]

    for side, near, far in ((0, 0, 1), (1, 7, 6)):
        for c in range(6):
            YS[side, c] = y_layer(c, near)
            YS[side, 8 + c] = y_layer(c, far)
        YS[side, 6] = PP[pl.ds(1, 8), TOP + near]
        YS[side, 7] = HP[pl.ds(1, 8), near, :].astype(f32)
        for s, xp in ((0, 2), (1, 9)):
            for c in range(6):
                ES[s, side, pl.ds(c, 1)] = VP[c, xp, pl.ds(TOP + near, 1)]

    pair = lane >> 1
    outer = jnp.where(odd, (lane + 1) >> 1, (lane >> 1) - 1) & 63
    near_z, far_z = zero, zero
    for c in range(8):
        one, two = zero, zero
        for x in range(8):
            if c < 6:
                plane = VP[c, x + 2, block]
            elif c == 6:
                plane = PP[x + 1, block]
            else:
                plane = HP[x + 1].astype(f32)
            k = 8 * c + x
            turned = roll(plane, 2 * k + 1, 1)
            one = jnp.where(pair == k, turned, one)
            if c < 6:
                two = jnp.where(outer == k, turned, two)
        near_z = jnp.where((lane >> 4) == c, one, near_z)
        if c < 6:
            far_z = jnp.where((outer >> 3) == c, two, far_z)
    WS[0] = far_z
    WS[1] = near_z
    near_zy = zero
    for side in range(2):
        for c in range(6):
            k = 8 * side + c
            near_zy = jnp.where(pair == k, roll(YS[side, c], 2 * k + 1, 1), near_zy)
    WS[2] = near_zy

    pl.semaphore_wait(barrier, sum(n.values()) - 3 + edges)
    for group in (x_near, y_near, z_face, xy_edge, xz_edge, yz_edge, x_far, y_far):
        start(group)

    picked = acc_ref[0]
    length = jnp.where(
        picked == 0, f32(1.0), jnp.where(picked == 1, f32(0.5), jnp.where(picked == 2, f32(0.25), f32(0.125)))
    )
    for c in range(3):
        for x in range(8):
            CV[c, x] = VP[c, x + 2, block] + length * VP[3 + c, x + 2, block]
    out_v = pltpu.make_async_copy(CV, cv_hbm, out_sem.at[0])
    out_v.start()

    full = lambda s: jnp.full((8, 128), s, f32)
    table = []
    for k in range(4):
        exponent = full(exp_ref[k])
        table.append((full(fac_ref[k]), (1.0 - exponent) / (2.0 * exponent), full(0.5 * yld_ref[k])))

    def params(ids):
        out = table[3]
        for k in (2, 1, 0):
            hit = ids == k
            out = tuple(jnp.where(hit, mine, other) for mine, other in zip(table[k], out))
        return out

    def tensor(g):
        return (
            g[0][0], g[1][1], g[2][2],
            0.5 * (g[0][1] + g[1][0]), 0.5 * (g[0][2] + g[2][0]), 0.5 * (g[1][2] + g[2][1]),
        )

    def dot(a, b):
        return (a[0] * b[0] + a[1] * b[1] + a[2] * b[2]) + 2.0 * (a[3] * b[3] + a[4] * b[4] + a[5] * b[5])

    def flow(second, factor, power, half_yield):
        inverse = lax.rsqrt(second)
        creep = factor * jnp.exp(power * jnp.log(second))
        plastic = half_yield * inverse
        total = creep + plastic
        return inverse, creep, plastic, total, creep * plastic / total

    def stresses(g, ids, wanted, mask=None):
        factor, power, half_yield = params(ids)
        base, change = tensor(g[:3]), tensor(g[3:])
        inverse, creep, plastic, total, harmonic = flow(0.125 * dot(base, base) + 0.01, factor, power, half_yield)
        viscosity = harmonic + 0.05
        slope = harmonic * (inverse * inverse) * (plastic * power - 0.5 * creep) / total
        along = slope * (0.25 * dot(base, change))
        if mask is not None:
            viscosity, along = viscosity * mask, along * mask
        fields = [
            {c: viscosity * base[c] for c in wanted},
            {c: viscosity * change[c] + along * base[c] for c in wanted},
        ]
        for a in LENGTHS:
            trial = tuple(e + f if a == 1.0 else e + a * f for e, f in zip(base, change))
            viscosity = flow(0.125 * dot(trial, trial) + 0.01, factor, power, half_yield)[4] + 0.05
            if mask is not None:
                viscosity = viscosity * mask
            fields.append({c: viscosity * trial[c] for c in wanted})
        return fields

    def across_z(plane, ends):
        return jnp.where(last_lane, ends, roll(plane, -1, 1)) - jnp.where(first_lane, ends, roll(plane, 1, 1))

    def ends_of(packed, k):
        return roll(packed, -(2 * k + 1), 1)

    def joined(below, above):
        return jnp.where(odd, roll(below, 1, 1), roll(above, -1, 1))

    def flag(a, s):
        return has[a, s].astype(f32)

    def plane_differences(xp, packed, x):
        g = []
        for c in range(6):
            centre = VP[c, xp, block]
            g.append((
                VP[c, xp + 1, block] - VP[c, xp - 1, block],
                VP[c, xp, pl.ds(TOP + 1, 8)] - VP[c, xp, pl.ds(TOP - 1, 8)],
                across_z(centre, ends_of(packed, 8 * c + x)),
            ))
        return g

    every = tuple(range(6))

    def store_plane(xs, fields):
        for f, field in enumerate(fields):
            for c, value in field.items():
                SS[f, c, xs, block] = value

    arrived(z_face)
    arrived(y_near)
    near_halo = joined(ZR[0, 1], ZR[1, 1])
    far_halo = jnp.where(odd, roll(ZR[0, 0], 2, 1), roll(ZR[1, 0], -2, 1))
    for side, row in ((0, TOP - 1), (1, TOP + 8)):
        for c in range(6):
            VP[c, pl.ds(2, 8), row] = YR[side, c]
        PP[pl.ds(1, 8), row] = YR[side, 6]
    for x in range(1, 7):
        store_plane(x + 1, stresses(plane_differences(x + 2, near_halo, x), HP[x + 1], every))

    arrived(x_near)
    for x in (0, 7):
        store_plane(x + 1, stresses(plane_differences(x + 2, near_halo, x), HP[x + 1], every))
    arrived(xy_edge)
    arrived(xz_edge)
    x_ends = [joined(XZ[side, 0, 0], XZ[side, 1, 0]) for side in range(2)]
    for s, xp in ((0, 1), (1, 10)):
        for t, row in ((0, TOP - 1), (1, TOP + 8)):
            for c in range(6):
                VP[c, xp, pl.ds(row, 1)] = ER[s, t, pl.ds(c, 1)]
    arrived(x_far)
    for side, xp, x in ((0, 1, 7), (1, 10, 0)):
        g = plane_differences(xp, x_ends[side], x)
        store_plane(xp - 1, stresses(g, HP[xp - 1], ALONG[0], flag("gx", 2 * side - 1)))

    arrived(yz_edge)
    arrived(y_far)
    for side in range(2):
        packed = joined(YZ[side, 0, 1], YZ[side, 1, 1])
        g = []
        for c in range(6):
            centre = YR[side, c]
            above = jnp.where(sub == 7, ER[1, side, pl.ds(c, 1)], roll(centre, -1, 0))
            below = jnp.where(sub == 0, ER[0, side, pl.ds(c, 1)], roll(centre, 1, 0))
            outward = YS[side, c] - YR[side, 8 + c]
            g.append((
                above - below,
                outward if side == 0 else -outward,
                across_z(centre, ends_of(packed, 8 * (1 - side) + c)),
            ))
        fields = stresses(g, YR[side, 7], ALONG[1], flag("gy", 2 * side - 1))
        row = TOP - 1 if side == 0 else TOP + 8
        for f, field in enumerate(fields):
            for c, value in field.items():
                SS[f, c, pl.ds(1, 8), row] = value

    inner = WS[1]
    y_ends = [joined(YZ[side, 0, 0], YZ[side, 1, 0]) for side in range(2)]
    column = pair & 7
    out_z = jnp.where(odd, inner - far_halo, far_halo - inner)
    out_y = roll(jnp.where(sub == 0, y_ends[1], near_halo), -1, 0) - roll(
        jnp.where(sub == 7, y_ends[0], near_halo), 1, 0
    )
    out_x = jnp.where(column == 7, roll(x_ends[1], 14, 1), roll(near_halo, -2, 1)) - jnp.where(
        column == 0, roll(x_ends[0], -14, 1), roll(near_halo, 2, 1)
    )
    g = [tuple(roll(o, -16 * c, 1) if c else o for o in (out_x, out_y, out_z)) for c in range(6)]
    mask = jnp.where(odd, flag("gz", -1), flag("gz", 1))
    z_fields = stresses(g, roll(near_halo, -112, 1), ALONG[2], mask)

    loads[4].wait()
    sums = [zero] * 8
    for x in range(8):
        xs = x + 1
        p_plane = PP[xs, block]
        slope = (
            PP[xs + 1, block] - PP[xs - 1, block],
            PP[xs, pl.ds(TOP + 1, 8)] - PP[xs, pl.ds(TOP - 1, 8)],
            across_z(p_plane, ends_of(near_halo, 48 + x)),
        )
        for i in range(3):
            loading = BF[i, x] - 0.5 * slope[i]
            cx, cy, cz = ALONG[0][i], ALONG[1][i], ALONG[2][i]
            out = []
            for f in range(6):
                change = SS[f, cx, xs + 1, block] - SS[f, cx, xs - 1, block]
                change = change + (SS[f, cy, xs, pl.ds(TOP + 1, 8)] - SS[f, cy, xs, pl.ds(TOP - 1, 8)])
                change = change + across_z(SS[f, cz, xs, block], ends_of(z_fields[f][cz], x))
                out.append(0.5 * change if f == 1 else 0.5 * change + loading)
            chosen = out[5]
            for k in (2, 1, 0):
                chosen = jnp.where(picked == k, out[2 + k], chosen)
            CR[i, x] = chosen
            for k, a in enumerate(LENGTHS):
                sums[k] = sums[k] + out[2 + k] * out[2 + k]
                linear = out[0] + a * out[1]
                sums[4 + k] = sums[4 + k] + linear * linear
    out_r = pltpu.make_async_copy(CR, cr_hbm, out_sem.at[1])
    out_r.start()

    stacked = zero
    for k in range(8):
        stacked = jnp.where(sub == k, jnp.sum(sums[k], axis=0, keepdims=True), stacked)
    totals = jnp.sum(stacked, axis=1, keepdims=True)
    row = jnp.sum(jnp.where(lane == sub, totals, 0.0), axis=0, keepdims=True)
    shares = []
    for a, ref, sems in (("gz", RZ, rz_sem), ("gx", RX, rx_sem), ("gy", RY, ry_sem)):
        mine = me[a]
        ref[mine] = row
        copies = []
        for k in range(1, n[a]):
            copies.append(
                pltpu.make_async_remote_copy(
                    src_ref=ref.at[mine], dst_ref=ref.at[mine], send_sem=sems.at[0, k], recv_sem=sems.at[1, k],
                    device_id={a: lax.rem(mine + k, n[a])}, device_id_type=MESH,
                )
            )
        for copy in copies:
            copy.start()
        for copy in copies:
            copy.wait_recv()
        row = ref[0]
        for k in range(1, n[a]):
            row = row + ref[k]
        shares += copies
    cells = 3.0 * (8 * n["gx"]) * (8 * n["gy"]) * (128 * n["gz"])
    norms = jnp.sqrt(row / cells + 1e-6)
    norms_ref[pl.ds(0, 1)] = norms[:, 0:4]
    norms_ref[pl.ds(1, 1)] = roll(jnp.broadcast_to(norms, (8, 128)), -4, 1)[0:1, 0:4]

    for copy in shares:
        copy.wait_send()
    for group in (x_near, y_near, z_face, xy_edge, xz_edge, yz_edge, x_far, y_far):
        sent(group)
    out_v.wait()
    out_r.wait()


def solution(mesh):
    sizes = tuple(mesh.shape[a] for a in ("gx", "gy", "gz"))
    f32 = jnp.float32

    def body(*args):
        vector = jax.ShapeDtypeStruct((3, 8, 8, 128), f32)
        anywhere = pl.BlockSpec(memory_space=pl.ANY)
        scalars = pl.BlockSpec(memory_space=pltpu.SMEM)
        return pl.pallas_call(
            functools.partial(kernel, sizes),
            out_shape=(jax.ShapeDtypeStruct((2, 4), f32), vector, vector),
            in_specs=[anywhere] * 5 + [scalars] * 4,
            out_specs=(pl.BlockSpec(memory_space=pltpu.VMEM), anywhere, anywhere),
            scratch_shapes=[
                pltpu.VMEM((6, 12, ROWS, 128), f32),
                pltpu.VMEM((10, ROWS, 128), f32),
                pltpu.VMEM((10, 8, 128), jnp.int32),
                pltpu.VMEM((3, 8, 8, 128), f32),
                pltpu.VMEM((2, 14, 8, 128), f32),
                pltpu.VMEM((2, 14, 8, 128), f32),
                pltpu.VMEM((3, 8, 128), f32),
                pltpu.VMEM((2, 2, 8, 128), f32),
                pltpu.VMEM((2, 2, 1, 8, 128), f32),
                pltpu.VMEM((2, 2, 2, 8, 128), f32),
                pltpu.VMEM((2, 2, 8, 128), f32),
                pltpu.VMEM((2, 2, 8, 128), f32),
                pltpu.VMEM((6, 6, 10, ROWS, 128), f32),
                pltpu.VMEM((3, 8, 8, 128), f32),
                pltpu.VMEM((3, 8, 8, 128), f32),
                pltpu.VMEM((sizes[2], 1, 128), f32),
                pltpu.VMEM((sizes[0], 1, 128), f32),
                pltpu.VMEM((sizes[1], 1, 128), f32),
                pltpu.SemaphoreType.DMA((5,)),
                pltpu.SemaphoreType.DMA((2,)),
                pltpu.SemaphoreType.DMA((26,)),
                pltpu.SemaphoreType.DMA((26,)),
                pltpu.SemaphoreType.DMA((2, sizes[2])),
                pltpu.SemaphoreType.DMA((2, sizes[0])),
                pltpu.SemaphoreType.DMA((2, sizes[1])),
            ],
            compiler_params=pltpu.CompilerParams(collective_id=0, has_side_effects=True),
            name="line_search",
        )(*args)

    vector, scalar = P(None, "gx", "gy", "gz"), P("gx", "gy", "gz")
    return jax.shard_map(
        body,
        mesh=mesh,
        in_specs=(vector, vector, scalar, vector, scalar, P(), P(), P(), P()),
        out_specs=(P(), vector, vector),
        check_vma=False,
    )
```

time: 152 us -> 39.6 us (0.26)
  blocking collectives: 50.4 us -> 0 us
  starting transfers between devices: 49.5 us -> 0 us
  Pallas kernels: 0 us -> 34.6 us
  other arithmetic: 21.8 us -> 0 us
  local copies, waits for them, and re-layouts: 16.6 us -> 3.41 us
  waiting for transfers between devices: 10.7 us -> 0 us
    psum x4 -> x0, blocking collectives: 50.4 us -> none  [over_axes(): array = lax.psum(array, axis)]
    ppermute x18 -> x0, starting transfers between devices: 49.5 us -> none  [the longest x6 22.1 us: extended(): before = lax.ppermute(last, axis, up)]
    pallas_call x0 -> x1, Pallas kernels: none -> 34.6 us  [body(): pl.pallas_call(functools.partial(kernel, sizes), out_shape=(jax.ShapeDtyp...]
    ppermute x18 -> x0, waiting for transfers between devices: 10.7 us -> none  [the longest x6 9.7 us: extended(): after = lax.ppermute(leading, axis, down)]
    mul x8 -> x0, other arithmetic: 8.76 us -> none  [the longest x2 3.93 us: stress_stack(): trial_stress = 2.0 * spread_cells(trial_viscosity) * trial_rates]
    another operation x5 -> x0, local copies, waits for them, and re-layouts: 5.31 us -> none  [the longest x1 4.97 us: body(): sums = over_axes(jnp.stack(actual + predicted), GX_GY_GZ)]
    slice x9 -> x0, local copies, waits for them, and re-layouts: 4.59 us -> none  [the longest x2 1.62 us: with_halo(): leading = lax.slice_in_dim(array, 0, width, axis=dim)]
    another operation x7 -> x0, other arithmetic: 4.54 us -> none  [the longest x1 1.81 us: body(): jnp.stack([paired[0] + length * paired[1] for length in step_lengths])]
  transfers between devices with their start and end apart: 18 -> 0, of which waited for: 4 -> 0; matrix products, arithmetic and copies ran while one was open for 5% -> 0% of each run, Pallas kernels for 0% -> 0%
where the time goes in v1:
time: 39.6 us; the launch traced here: 39.3 us
  Pallas kernels  34.6 us (87%)
  local copies, waits for them, and re-layouts  3.41 us (9%)
  between operations  1.3 us (3%)
    pallas_call x1, Pallas kernels, body(): pl.pallas_call(functools.partial(kernel, sizes), out_shape=(jax.ShapeDtyp...  34.6 us
    unnamed x7, local copies, waits for them, and re-layouts  3.41 us

profile of v1, /device:TPU:1, one launch (start us, length us, event | category | flops | bytes accessed | tf_op | source)
XLA Modules:
  0.0 39.3 jit_solution(13542272932105867314)
XLA Ops:
  1.3 34.6 %line_search.1 = (f32[2,4]{1,0:T(2,128)}, f32[3,8,8,128]{3,2,1,0:T(8,128)}, f32[3,8,8,128]{3,2,1,0:T(8,128)}) custom-call(f32[3,8,8,128]{3,2,1,0:T(8,128)} %v_hbm.1, f32[3,8,8,128]{3,2,1,0:T(8,128)} %d_hbm.1, f32[8,8,128]{2,1,0:T(8,128)} %p_hbm.1, f32[3,8,8,128]{3,2,1,0:T(8,128)} %b_hbm.1, s32[8,8,128]{2,1,0:T(8,128)} %ph_hbm.1, f32[4]{0:T(128)} %fac_ref.1, ...), custom_call_target="tpu_custom_call" | custom-call | tf_op jit(solution)/shard_map/line_search/pallas_call | solution.py:415
  35.9 0.0 copy-start.1
  35.9 0.6 %copy-done.1 = f32[2,4]{1,0:T(2,128)S(1)} copy-done((f32[2,4]{1,0:T(2,128)S(1)}, f32[2,4]{1,0:T(2,128)}, u32[]{:S(2)}) %copy-start.1) | copy-done | bytes 56
  36.6 0.6 %copy.16 = f32[2,4]{1,0:T(2,128)} copy(f32[2,4]{1,0:T(2,128)S(1)} %copy-done.1) | data formatting | bytes 64
  37.1 0.0 copy-start
  37.1 1.6 %copy.17 = f32[3,8,8,128]{3,2,1,0:T(8,128)} copy(f32[3,8,8,128]{3,2,1,0:T(8,128)} %get-tuple-element.7) | data formatting | bytes 196608
  38.7 0.0 copy-done
  38.7 0.6 %copy.18 = f32[3,8,8,128]{3,2,1,0:T(8,128)} copy(f32[3,8,8,128]{3,2,1,0:T(8,128)S(1)} %copy-done) | data formatting | bytes 196608
Async XLA Ops:
  35.9 0.6 %copy-start.1 = (f32[2,4]{1,0:T(2,128)S(1)}, f32[2,4]{1,0:T(2,128)}, u32[]{:S(2)}) copy-start(f32[2,4]{1,0:T(2,128)} %get-tuple-element.6) | copy-start | bytes 100
  37.1 1.6 %copy-start = (f32[3,8,8,128]{3,2,1,0:T(8,128)S(1)}, f32[3,8,8,128]{3,2,1,0:T(8,128)}, u32[]{:S(2)}) copy-start(f32[3,8,8,128]{3,2,1,0:T(8,128)} %get-tuple-element.8) | copy-start | bytes 294916

commit v2 on v1

--- a/solution.py
+++ b/solution.py
@@ -20,10 +20,10 @@
 
 def kernel(
     sizes,
-    v_hbm, d_hbm, p_hbm, b_hbm, ph_hbm, fac_ref, exp_ref, yld_ref, acc_ref,
-    norms_ref, cv_hbm, cr_hbm,
-    VP, PP, HP, BF, YS, YR, WS, ZR, XZ, YZ, ES, ER, SS, CV, CR, RZ, RX, RY,
-    load_sem, out_sem, send_sem, recv_sem, rz_sem, rx_sem, ry_sem,
+    v_hbm, d_hbm, p_hbm, b_hbm, ph_hbm, fac_hbm, exp_hbm, yld_hbm, acc_ref,
+    norms_ref, CV, CR,
+    fac_ref, exp_ref, yld_ref, VP, PP, HP, BF, YS, YR, WS, ZR, XZ, YZ, ES, ER, SS, RZ, RX, RY,
+    load_sem, send_sem, recv_sem, rz_sem, rx_sem, ry_sem,
 ):
     n = dict(zip(("gx", "gy", "gz"), sizes))
     me = {a: lax.axis_index(a) for a in n}
@@ -44,6 +44,9 @@
         pltpu.make_async_copy(p_hbm, PP.at[pl.ds(1, 8), block], load_sem.at[2]),
         pltpu.make_async_copy(ph_hbm, HP.at[pl.ds(1, 8)], load_sem.at[3]),
         pltpu.make_async_copy(b_hbm, BF, load_sem.at[4]),
+        pltpu.make_async_copy(fac_hbm, fac_ref, load_sem.at[5]),
+        pltpu.make_async_copy(exp_hbm, exp_ref, load_sem.at[6]),
+        pltpu.make_async_copy(yld_hbm, yld_ref, load_sem.at[7]),
     ]
     for load in loads:
         load.start()
@@ -122,9 +125,6 @@
             xy_edge.append(message({"gx": s, "gy": t}, [(ES.at[hi(s), hi(t)], ER.at[lo(s), lo(t)])]))
 
     barrier = pltpu.get_barrier_semaphore()
-    for a in n:
-        for k in range(1, n[a]):
-            pl.semaphore_signal(barrier, inc=1, device_id={a: lax.rem(me[a] + k, n[a])}, device_id_type=MESH)
     for a, b in (("gx", "gy"), ("gx", "gz"), ("gy", "gz")):
         for s in both:
             for t in both:
@@ -133,6 +133,9 @@
                     pl.semaphore_signal(
                         barrier, inc=1, device_id={a: me[a] + s, b: me[b] + t}, device_id_type=MESH
                     )
+    for a in n:
+        for k in sorted(range(1, n[a]), key=lambda k: min(k, n[a] - k)):
+            pl.semaphore_signal(barrier, inc=1, device_id={a: lax.rem(me[a] + k, n[a])}, device_id_type=MESH)
     sides = {a: has[a, 1].astype(jnp.int32) + has[a, -1].astype(jnp.int32) for a in n}
     edges = sides["gx"] * sides["gy"] + sides["gx"] * sides["gz"] + sides["gy"] * sides["gz"]
 
@@ -185,6 +188,8 @@
     for group in (x_near, y_near, z_face, xy_edge, xz_edge, yz_edge, x_far, y_far):
         start(group)
 
+    for load in loads[5:]:
+        load.wait()
     picked = acc_ref[0]
     length = jnp.where(
         picked == 0, f32(1.0), jnp.where(picked == 1, f32(0.5), jnp.where(picked == 2, f32(0.25), f32(0.125)))
@@ -192,8 +197,6 @@
     for c in range(3):
         for x in range(8):
             CV[c, x] = VP[c, x + 2, block] + length * VP[3 + c, x + 2, block]
-    out_v = pltpu.make_async_copy(CV, cv_hbm, out_sem.at[0])
-    out_v.start()
 
     full = lambda s: jnp.full((8, 128), s, f32)
     table = []
@@ -363,8 +366,6 @@
                 sums[k] = sums[k] + out[2 + k] * out[2 + k]
                 linear = out[0] + a * out[1]
                 sums[4 + k] = sums[4 + k] + linear * linear
-    out_r = pltpu.make_async_copy(CR, cr_hbm, out_sem.at[1])
-    out_r.start()
 
     stacked = zero
     for k in range(8):
@@ -400,8 +401,14 @@
         copy.wait_send()
     for group in (x_near, y_near, z_face, xy_edge, xz_edge, yz_edge, x_far, y_far):
         sent(group)
-    out_v.wait()
-    out_r.wait()
+
+
+def write_out(*refs):
+    copies = [pltpu.make_async_copy(refs[i], refs[3 + i], refs[6].at[i]) for i in range(3)]
+    for copy in copies:
+        copy.start()
+    for copy in copies:
+        copy.wait()
 
 
 def solution(mesh):
@@ -411,13 +418,18 @@
     def body(*args):
         vector = jax.ShapeDtypeStruct((3, 8, 8, 128), f32)
         anywhere = pl.BlockSpec(memory_space=pl.ANY)
-        scalars = pl.BlockSpec(memory_space=pltpu.SMEM)
-        return pl.pallas_call(
+        inside = pl.BlockSpec(memory_space=pltpu.VMEM)
+        args = [pltpu.with_memory_space_constraint(a, pltpu.HBM) for a in args[:8]] + [args[8]]
+        outputs = (jax.ShapeDtypeStruct((2, 4), f32), vector, vector)
+        found = pl.pallas_call(
             functools.partial(kernel, sizes),
-            out_shape=(jax.ShapeDtypeStruct((2, 4), f32), vector, vector),
-            in_specs=[anywhere] * 5 + [scalars] * 4,
-            out_specs=(pl.BlockSpec(memory_space=pltpu.VMEM), anywhere, anywhere),
+            out_shape=outputs,
+            in_specs=[pl.BlockSpec(memory_space=pltpu.HBM)] * 8 + [pl.BlockSpec(memory_space=pltpu.SMEM)],
+            out_specs=(inside,) * 3,
             scratch_shapes=[
+                pltpu.SMEM((4,), f32),
+                pltpu.SMEM((4,), f32),
+                pltpu.SMEM((4,), f32),
                 pltpu.VMEM((6, 12, ROWS, 128), f32),
                 pltpu.VMEM((10, ROWS, 128), f32),
                 pltpu.VMEM((10, 8, 128), jnp.int32),
@@ -431,22 +443,30 @@
                 pltpu.VMEM((2, 2, 8, 128), f32),
                 pltpu.VMEM((2, 2, 8, 128), f32),
                 pltpu.VMEM((6, 6, 10, ROWS, 128), f32),
-                pltpu.VMEM((3, 8, 8, 128), f32),
-                pltpu.VMEM((3, 8, 8, 128), f32),
                 pltpu.VMEM((sizes[2], 1, 128), f32),
                 pltpu.VMEM((sizes[0], 1, 128), f32),
                 pltpu.VMEM((sizes[1], 1, 128), f32),
-                pltpu.SemaphoreType.DMA((5,)),
-                pltpu.SemaphoreType.DMA((2,)),
+                pltpu.SemaphoreType.DMA((8,)),
                 pltpu.SemaphoreType.DMA((26,)),
                 pltpu.SemaphoreType.DMA((26,)),
                 pltpu.SemaphoreType.DMA((2, sizes[2])),
                 pltpu.SemaphoreType.DMA((2, sizes[0])),
                 pltpu.SemaphoreType.DMA((2, sizes[1])),
             ],
-            compiler_params=pltpu.CompilerParams(collective_id=0, has_side_effects=True),
+            compiler_params=pltpu.CompilerParams(
+                collective_id=0, has_side_effects=True, vmem_limit_bytes=16 * 1024 * 1024
+            ),
             name="line_search",
         )(*args)
+        return pl.pallas_call(
+            write_out,
+            out_shape=outputs,
+            in_specs=[inside] * 3,
+            out_specs=(anywhere,) * 3,
+            scratch_shapes=[pltpu.SemaphoreType.DMA((3,))],
+            compiler_params=pltpu.CompilerParams(vmem_limit_bytes=4 * 1024 * 1024),
+            name="write_out",
+        )(*found)
 
     vector, scalar = P(None, "gx", "gy", "gz"), P("gx", "gy", "gz")
     return jax.shard_map(

time: 39.6 us -> 35.7 us (0.902)
  local copies, waits for them, and re-layouts: 3.41 us -> 0 us
  Pallas kernels: 34.6 us -> 34.2 us
    unnamed x7 -> x0, local copies, waits for them, and re-layouts: 3.41 us -> none
    pallas_call x1 -> x2, Pallas kernels: 34.6 us -> 34.2 us  [the longest x1 33.5 us: body(): pl.pallas_call(functools.partial(kernel, sizes), out_shape=outputs, in_sp...]
where the time goes in v2:
time: 35.7 us; the launch traced here: 35.5 us
  Pallas kernels  34.2 us (96%)
  between operations  1.29 us (4%)
    pallas_call x1, Pallas kernels, body(): pl.pallas_call(functools.partial(kernel, sizes), out_shape=outputs, in_sp...  33.5 us

profile of v2, /device:TPU:1, one launch (start us, length us, event | category | flops | bytes accessed | tf_op | source)
XLA Modules:
  0.0 35.5 jit_solution(13567481214994035218)
XLA Ops:
  1.3 33.5 %line_search.1 = (f32[2,4]{1,0:T(2,128)S(1)}, f32[3,8,8,128]{3,2,1,0:T(8,128)S(1)}, f32[3,8,8,128]{3,2,1,0:T(8,128)S(1)}) custom-call(f32[3,8,8,128]{3,2,1,0:T(8,128)} %v_hbm.1, f32[3,8,8,128]{3,2,1,0:T(8,128)} %d_hbm.1, f32[8,8,128]{2,1,0:T(8,128)} %p_hbm.1, f32[3,8,8,128]{3,2,1,0:T(8,128)} %b_hbm.1, s32[8,8,128]{2,1,0:T(8,128)} %ph_hbm.1, f32[4]{0:T(128)} %fac_hbm.1, ...), custom_call_target="tpu_custom_call" | custom-call | tf_op jit(solution)/shard_map/line_search/pallas_call | solution.py:424
  34.8 0.7 %write_out.1 = (f32[2,4]{1,0:T(2,128)}, f32[3,8,8,128]{3,2,1,0:T(8,128)}, f32[3,8,8,128]{3,2,1,0:T(8,128)}) custom-call(f32[2,4]{1,0:T(2,128)S(1)} %get-tuple-element.6.refs_0_, f32[3,8,8,128]{3,2,1,0:T(8,128)S(1)} %get-tuple-element.7.refs_1_, f32[3,8,8,128]{3,2,1,0:T(8,128)S(1)} %get-tuple-element.8.refs_2_), custom_call_target="tpu_custom_call" | custom-call | tf_op jit(solution)/shard_map/write_out/pallas_call | solution.py:461

commit v3 on v2

--- a/solution.py
+++ b/solution.py
@@ -18,12 +18,32 @@
     return pltpu.roll(values, shift % values.shape[axis], axis)
 
 
+def known_rounds(sizes):
+    def steps(size):
+        found, step = [], 1
+        while step < size // 2:
+            found.append(step)
+            step *= 2
+        return found
+
+    x, y, z = sizes
+    chains = ([("gz", k) for k in steps(z)], [("gx", k) for k in steps(x)] + [("gy", 1)] + [("gy", k) for k in steps(y)])
+    rounds, counted = [], 0
+    for r in range(max(len(c) for c in chains)):
+        rounds.append([])
+        for c in chains:
+            if r < len(c):
+                rounds[-1].append((counted,) + c[r])
+                counted += 1
+    return rounds
+
+
 def kernel(
     sizes,
     v_hbm, d_hbm, p_hbm, b_hbm, ph_hbm, fac_hbm, exp_hbm, yld_hbm, acc_ref,
     norms_ref, CV, CR,
-    fac_ref, exp_ref, yld_ref, VP, PP, HP, BF, YS, YR, WS, ZR, XZ, YZ, ES, ER, SS, RZ, RX, RY,
-    load_sem, send_sem, recv_sem, rz_sem, rx_sem, ry_sem,
+    fac_ref, exp_ref, yld_ref, VP, PP, HP, BF, YS, YR, WS, ZR, XZ, YZ, ES, ER, SS, RZ, RP,
+    load_sem, send_sem, recv_sem, rz_sem, rp_sem, know_sem,
 ):
     n = dict(zip(("gx", "gy", "gz"), sizes))
     me = {a: lax.axis_index(a) for a in n}
@@ -125,6 +145,13 @@
             xy_edge.append(message({"gx": s, "gy": t}, [(ES.at[hi(s), hi(t)], ER.at[lo(s), lo(t)])]))
 
     barrier = pltpu.get_barrier_semaphore()
+
+    def ring(a, step):
+        return {a: lax.rem(me[a] + step + n[a], n[a])}
+
+    for a in n:
+        for s in both:
+            pl.semaphore_signal(barrier, inc=1, device_id=ring(a, s), device_id_type=MESH)
     for a, b in (("gx", "gy"), ("gx", "gz"), ("gy", "gz")):
         for s in both:
             for t in both:
@@ -133,11 +160,25 @@
                     pl.semaphore_signal(
                         barrier, inc=1, device_id={a: me[a] + s, b: me[b] + t}, device_id_type=MESH
                     )
-    for a in n:
-        for k in sorted(range(1, n[a]), key=lambda k: min(k, n[a] - k)):
-            pl.semaphore_signal(barrier, inc=1, device_id={a: lax.rem(me[a] + k, n[a])}, device_id_type=MESH)
     sides = {a: has[a, 1].astype(jnp.int32) + has[a, -1].astype(jnp.int32) for a in n}
     edges = sides["gx"] * sides["gy"] + sides["gx"] * sides["gz"] + sides["gy"] * sides["gz"]
+
+    rounds = known_rounds(sizes)
+
+    def tell(r):
+        for i, a, step in rounds[r]:
+            for s in both:
+                pl.semaphore_signal(know_sem.at[i], inc=1, device_id=ring(a, s * step), device_id_type=MESH)
+
+    def told(r):
+        for i, _, _ in rounds[r]:
+            pl.semaphore_wait(know_sem.at[i], 2)
+
+    def learn(r):
+        if r < len(rounds):
+            told(r)
+            if r + 1 < len(rounds):
+                tell(r + 1)
 
     for load in loads[:4]:
         load.wait()
@@ -184,9 +225,11 @@
             near_zy = jnp.where(pair == k, roll(YS[side, c], 2 * k + 1, 1), near_zy)
     WS[2] = near_zy
 
-    pl.semaphore_wait(barrier, sum(n.values()) - 3 + edges)
+    pl.semaphore_wait(barrier, 6 + edges)
     for group in (x_near, y_near, z_face, xy_edge, xz_edge, yz_edge, x_far, y_far):
         start(group)
+    if rounds:
+        tell(0)
 
     for load in loads[5:]:
         load.wait()
@@ -278,6 +321,8 @@
             for c, value in field.items():
                 SS[f, c, xs, block] = value
 
+    learn(0)
+    learn(1)
     arrived(z_face)
     arrived(y_near)
     near_halo = joined(ZR[0, 1], ZR[1, 1])
@@ -288,6 +333,8 @@
         PP[pl.ds(1, 8), row] = YR[side, 6]
     for x in range(1, 7):
         store_plane(x + 1, stresses(plane_differences(x + 2, near_halo, x), HP[x + 1], every))
+
+    learn(2)
 
     arrived(x_near)
     for x in (0, 7):
@@ -338,6 +385,9 @@
     g = [tuple(roll(o, -16 * c, 1) if c else o for o in (out_x, out_y, out_z)) for c in range(6)]
     mask = jnp.where(odd, flag("gz", -1), flag("gz", 1))
     z_fields = stresses(g, roll(near_halo, -112, 1), ALONG[2], mask)
+
+    for r in range(3, len(rounds)):
+        learn(r)
 
     loads[4].wait()
     sums = [zero] * 8
@@ -373,24 +423,34 @@
     totals = jnp.sum(stacked, axis=1, keepdims=True)
     row = jnp.sum(jnp.where(lane == sub, totals, 0.0), axis=0, keepdims=True)
     shares = []
-    for a, ref, sems in (("gz", RZ, rz_sem), ("gx", RX, rx_sem), ("gy", RY, ry_sem)):
-        mine = me[a]
+    for axes, ref, sems in ((("gz",), RZ, rz_sem), (("gx", "gy"), RP, rp_sem)):
+        offsets = [()]
+        for a in axes:
+            offsets = [o + (k,) for o in offsets for k in range(n[a])]
+        hops = lambda o: sum(min(k, n[a] - k) for k, a in zip(o, axes))
+        mine = 0
+        for a in axes:
+            mine = mine * n[a] + me[a]
         ref[mine] = row
         copies = []
-        for k in range(1, n[a]):
-            copies.append(
-                pltpu.make_async_remote_copy(
-                    src_ref=ref.at[mine], dst_ref=ref.at[mine], send_sem=sems.at[0, k], recv_sem=sems.at[1, k],
-                    device_id={a: lax.rem(mine + k, n[a])}, device_id_type=MESH,
+        for i, o in sorted(enumerate(offsets), key=lambda item: -hops(item[1])):
+            if any(o):
+                copies.append(
+                    pltpu.make_async_remote_copy(
+                        src_ref=ref.at[mine], dst_ref=ref.at[mine],
+                        send_sem=sems.at[0, i], recv_sem=sems.at[1, i],
+                        device_id={a: lax.rem(me[a] + k, n[a]) for k, a in zip(o, axes)},
+                        device_id_type=MESH,
+                    )
                 )
-            )
         for copy in copies:
             copy.start()
         for copy in copies:
             copy.wait_recv()
-        row = ref[0]
-        for k in range(1, n[a]):
-            row = row + ref[k]
+        rows = [ref[k] for k in range(len(offsets))]
+        while len(rows) > 1:
+            rows = [sum(rows[k:k + 2]) for k in range(0, len(rows), 2)]
+        row = rows[0]
         shares += copies
     cells = 3.0 * (8 * n["gx"]) * (8 * n["gy"]) * (128 * n["gz"])
     norms = jnp.sqrt(row / cells + 1e-6)
@@ -444,14 +504,13 @@
                 pltpu.VMEM((2, 2, 8, 128), f32),
                 pltpu.VMEM((6, 6, 10, ROWS, 128), f32),
                 pltpu.VMEM((sizes[2], 1, 128), f32),
-                pltpu.VMEM((sizes[0], 1, 128), f32),
-                pltpu.VMEM((sizes[1], 1, 128), f32),
+                pltpu.VMEM((sizes[0] * sizes[1], 1, 128), f32),
                 pltpu.SemaphoreType.DMA((8,)),
                 pltpu.SemaphoreType.DMA((26,)),
                 pltpu.SemaphoreType.DMA((26,)),
                 pltpu.SemaphoreType.DMA((2, sizes[2])),
-                pltpu.SemaphoreType.DMA((2, sizes[0])),
-                pltpu.SemaphoreType.DMA((2, sizes[1])),
+                pltpu.SemaphoreType.DMA((2, sizes[0] * sizes[1])),
+                pltpu.SemaphoreType.REGULAR((max(1, sum(len(r) for r in known_rounds(sizes))),)),
             ],
             compiler_params=pltpu.CompilerParams(
                 collective_id=0, has_side_effects=True, vmem_limit_bytes=16 * 1024 * 1024

time: 35.7 us -> 35 us (0.980)
  Pallas kernels: 34.2 us -> 33.5 us
    pallas_call x1, Pallas kernels: 33.5 us -> 32.8 us  [body(): pl.pallas_call(functools.partial(kernel, sizes), out_shape=outputs, in_sp...]
where the time goes in v3:
time: 35 us; the launch traced here: 34.8 us
  Pallas kernels  33.5 us (96%)
  between operations  1.29 us (4%)
    pallas_call x1, Pallas kernels, body(): pl.pallas_call(functools.partial(kernel, sizes), out_shape=outputs, in_sp...  32.8 us
    pallas_call x1, Pallas kernels, body(): pl.pallas_call(write_out, out_shape=outputs, in_specs=[inside] * 3, out_s...  0.71 us

profile of v3, /device:TPU:1, one launch (start us, length us, event | category | flops | bytes accessed | tf_op | source)
XLA Modules:
  0.0 34.8 jit_solution(9668344960300743503)
XLA Ops:
  1.3 32.8 %line_search.1 = (f32[2,4]{1,0:T(2,128)S(1)}, f32[3,8,8,128]{3,2,1,0:T(8,128)S(1)}, f32[3,8,8,128]{3,2,1,0:T(8,128)S(1)}) custom-call(f32[3,8,8,128]{3,2,1,0:T(8,128)} %v_hbm.1, f32[3,8,8,128]{3,2,1,0:T(8,128)} %d_hbm.1, f32[8,8,128]{2,1,0:T(8,128)} %p_hbm.1, f32[3,8,8,128]{3,2,1,0:T(8,128)} %b_hbm.1, s32[8,8,128]{2,1,0:T(8,128)} %ph_hbm.1, f32[4]{0:T(128)} %fac_hbm.1, ...), custom_call_target="tpu_custom_call" | custom-call | tf_op jit(solution)/shard_map/line_search/pallas_call | solution.py:484
  34.1 0.7 %write_out.1 = (f32[2,4]{1,0:T(2,128)}, f32[3,8,8,128]{3,2,1,0:T(8,128)}, f32[3,8,8,128]{3,2,1,0:T(8,128)}) custom-call(f32[2,4]{1,0:T(2,128)S(1)} %get-tuple-element.6.refs_0_, f32[3,8,8,128]{3,2,1,0:T(8,128)S(1)} %get-tuple-element.7.refs_1_, f32[3,8,8,128]{3,2,1,0:T(8,128)S(1)} %get-tuple-element.8.refs_2_), custom_call_target="tpu_custom_call" | custom-call | tf_op jit(solution)/shard_map/write_out/pallas_call | solution.py:520

commit v4 on v3

--- a/solution.py
+++ b/solution.py
@@ -18,24 +18,11 @@
     return pltpu.roll(values, shift % values.shape[axis], axis)
 
 
-def known_rounds(sizes):
-    def steps(size):
-        found, step = [], 1
-        while step < size // 2:
-            found.append(step)
-            step *= 2
-        return found
-
-    x, y, z = sizes
-    chains = ([("gz", k) for k in steps(z)], [("gx", k) for k in steps(x)] + [("gy", 1)] + [("gy", k) for k in steps(y)])
-    rounds, counted = [], 0
-    for r in range(max(len(c) for c in chains)):
-        rounds.append([])
-        for c in chains:
-            if r < len(c):
-                rounds[-1].append((counted,) + c[r])
-                counted += 1
-    return rounds
+def reach(size, far):
+    return sorted((k for k in range(1, size) if min(k, size - k) <= far), key=lambda k: min(k, size - k))
+
+
+FAR = {"gx": 2, "gy": 2, "gz": 4}
 
 
 def kernel(
@@ -146,12 +133,15 @@
 
     barrier = pltpu.get_barrier_semaphore()
 
-    def ring(a, step):
-        return {a: lax.rem(me[a] + step + n[a], n[a])}
+    greeted = {a: reach(n[a], FAR[a]) for a in n}
+
+    def signal(sem, a, k):
+        pl.semaphore_signal(sem, inc=1, device_id={a: lax.rem(me[a] + k, n[a])}, device_id_type=MESH)
 
     for a in n:
-        for s in both:
-            pl.semaphore_signal(barrier, inc=1, device_id=ring(a, s), device_id_type=MESH)
+        for k in greeted[a]:
+            if k in (1, n[a] - 1):
+                signal(barrier, a, k)
     for a, b in (("gx", "gy"), ("gx", "gz"), ("gy", "gz")):
         for s in both:
             for t in both:
@@ -160,25 +150,15 @@
                     pl.semaphore_signal(
                         barrier, inc=1, device_id={a: me[a] + s, b: me[b] + t}, device_id_type=MESH
                     )
+    for a in n:
+        for k in greeted[a]:
+            if k not in (1, n[a] - 1):
+                signal(barrier, a, k)
     sides = {a: has[a, 1].astype(jnp.int32) + has[a, -1].astype(jnp.int32) for a in n}
     edges = sides["gx"] * sides["gy"] + sides["gx"] * sides["gz"] + sides["gy"] * sides["gz"]
 
-    rounds = known_rounds(sizes)
-
-    def tell(r):
-        for i, a, step in rounds[r]:
-            for s in both:
-                pl.semaphore_signal(know_sem.at[i], inc=1, device_id=ring(a, s * step), device_id_type=MESH)
-
-    def told(r):
-        for i, _, _ in rounds[r]:
-            pl.semaphore_wait(know_sem.at[i], 2)
-
-    def learn(r):
-        if r < len(rounds):
-            told(r)
-            if r + 1 < len(rounds):
-                tell(r + 1)
+    ends = [(a, k) for a in ("gz", "gx") for k in greeted[a] if len(greeted[a]) < n[a] - 1 and min(k, n[a] - k) == FAR[a]]
+    lines = [("gy", k) for k in greeted["gy"]]
 
     for load in loads[:4]:
         load.wait()
@@ -225,11 +205,11 @@
             near_zy = jnp.where(pair == k, roll(YS[side, c], 2 * k + 1, 1), near_zy)
     WS[2] = near_zy
 
-    pl.semaphore_wait(barrier, 6 + edges)
+    pl.semaphore_wait(barrier, sum(len(ks) for ks in greeted.values()) + edges)
     for group in (x_near, y_near, z_face, xy_edge, xz_edge, yz_edge, x_far, y_far):
         start(group)
-    if rounds:
-        tell(0)
+    for a, k in ends:
+        signal(know_sem.at[0], a, k)
 
     for load in loads[5:]:
         load.wait()
@@ -321,8 +301,6 @@
             for c, value in field.items():
                 SS[f, c, xs, block] = value
 
-    learn(0)
-    learn(1)
     arrived(z_face)
     arrived(y_near)
     near_halo = joined(ZR[0, 1], ZR[1, 1])
@@ -333,8 +311,6 @@
         PP[pl.ds(1, 8), row] = YR[side, 6]
     for x in range(1, 7):
         store_plane(x + 1, stresses(plane_differences(x + 2, near_halo, x), HP[x + 1], every))
-
-    learn(2)
 
     arrived(x_near)
     for x in (0, 7):
@@ -386,8 +362,10 @@
     mask = jnp.where(odd, flag("gz", -1), flag("gz", 1))
     z_fields = stresses(g, roll(near_halo, -112, 1), ALONG[2], mask)
 
-    for r in range(3, len(rounds)):
-        learn(r)
+    if ends:
+        pl.semaphore_wait(know_sem.at[0], len(ends))
+    for a, k in lines:
+        signal(know_sem.at[1], a, k)
 
     loads[4].wait()
     sums = [zero] * 8
@@ -432,6 +410,8 @@
         for a in axes:
             mine = mine * n[a] + me[a]
         ref[mine] = row
+        if len(axes) == 2:
+            pl.semaphore_wait(know_sem.at[1], len(lines))
         copies = []
         for i, o in sorted(enumerate(offsets), key=lambda item: -hops(item[1])):
             if any(o):
@@ -510,7 +490,7 @@
                 pltpu.SemaphoreType.DMA((26,)),
                 pltpu.SemaphoreType.DMA((2, sizes[2])),
                 pltpu.SemaphoreType.DMA((2, sizes[0] * sizes[1])),
-                pltpu.SemaphoreType.REGULAR((max(1, sum(len(r) for r in known_rounds(sizes))),)),
+                pltpu.SemaphoreType.REGULAR((2,)),
             ],
             compiler_params=pltpu.CompilerParams(
                 collective_id=0, has_side_effects=True, vmem_limit_bytes=16 * 1024 * 1024

time: 35 us -> 33.1 us (0.946)
  Pallas kernels: 33.5 us -> 31.7 us
    pallas_call x1, Pallas kernels: 32.8 us -> 31 us  [body(): pl.pallas_call(functools.partial(kernel, sizes), out_shape=outputs, in_sp...]
where the time goes in v4:
time: 33.1 us; the launch traced here: 32.9 us
  Pallas kernels  31.7 us (96%)
  between operations  1.29 us (4%)
    pallas_call x1, Pallas kernels, body(): pl.pallas_call(functools.partial(kernel, sizes), out_shape=outputs, in_sp...  31 us
    pallas_call x1, Pallas kernels, body(): pl.pallas_call(write_out, out_shape=outputs, in_specs=[inside] * 3, out_s...  0.71 us

profile of v4, /device:TPU:1, one launch (start us, length us, event | category | flops | bytes accessed | tf_op | source)
XLA Modules:
  0.0 32.9 jit_solution(7342020511592846832)
XLA Ops:
  1.3 31.0 %line_search.1 = (f32[2,4]{1,0:T(2,128)S(1)}, f32[3,8,8,128]{3,2,1,0:T(8,128)S(1)}, f32[3,8,8,128]{3,2,1,0:T(8,128)S(1)}) custom-call(f32[3,8,8,128]{3,2,1,0:T(8,128)} %v_hbm.1, f32[3,8,8,128]{3,2,1,0:T(8,128)} %d_hbm.1, f32[8,8,128]{2,1,0:T(8,128)} %p_hbm.1, f32[3,8,8,128]{3,2,1,0:T(8,128)} %b_hbm.1, s32[8,8,128]{2,1,0:T(8,128)} %ph_hbm.1, f32[4]{0:T(128)} %fac_hbm.1, ...), custom_call_target="tpu_custom_call" | custom-call | tf_op jit(solution)/shard_map/line_search/pallas_call | solution.py:464
  32.2 0.7 %write_out.1 = (f32[2,4]{1,0:T(2,128)}, f32[3,8,8,128]{3,2,1,0:T(8,128)}, f32[3,8,8,128]{3,2,1,0:T(8,128)}) custom-call(f32[2,4]{1,0:T(2,128)S(1)} %get-tuple-element.6.refs_0_, f32[3,8,8,128]{3,2,1,0:T(8,128)S(1)} %get-tuple-element.7.refs_1_, f32[3,8,8,128]{3,2,1,0:T(8,128)S(1)} %get-tuple-element.8.refs_2_), custom_call_target="tpu_custom_call" | custom-call | tf_op jit(solution)/shard_map/write_out/pallas_call | solution.py:500

commit v5 on v4

--- a/solution.py
+++ b/solution.py
@@ -11,6 +11,7 @@
 LENGTHS = (1.0, 0.5, 0.25, 0.125)
 ROWS = 24
 TOP = 8
+TOGETHER = 6
 ALONG = ((0, 3, 4), (3, 1, 5), (4, 5, 2))
 
 
@@ -22,15 +23,28 @@
     return sorted((k for k in range(1, size) if min(k, size - k) <= far), key=lambda k: min(k, size - k))
 
 
-FAR = {"gx": 2, "gy": 2, "gz": 4}
+def doubling(step, end):
+    found = []
+    while step < end:
+        found.append(step)
+        step *= 2
+    return found
+
+
+def take_rows(ref, start, row):
+    return ref.reshape(ref.shape[0] * ROWS, 128)[pl.ds(start * ROWS + row, 8, stride=ROWS), :]
+
+
+def put_rows(ref, start, row, value):
+    ref.reshape(ref.shape[0] * ROWS, 128)[pl.ds(start * ROWS + row, 8, stride=ROWS), :] = value
 
 
 def kernel(
     sizes,
     v_hbm, d_hbm, p_hbm, b_hbm, ph_hbm, fac_hbm, exp_hbm, yld_hbm, acc_ref,
     norms_ref, CV, CR,
-    fac_ref, exp_ref, yld_ref, VP, PP, HP, BF, YS, YR, WS, ZR, XZ, YZ, ES, ER, SS, RZ, RP,
-    load_sem, send_sem, recv_sem, rz_sem, rp_sem, know_sem,
+    fac_ref, exp_ref, yld_ref, VP, PP, HP, BF, YS, YR, WS, ZR, XZ, YZ, ES, ER, SS, PR, RZ, RP,
+    load_sem, send_sem, recv_sem, sum_sem, know_sem,
 ):
     n = dict(zip(("gx", "gy", "gz"), sizes))
     me = {a: lax.axis_index(a) for a in n}
@@ -46,14 +60,14 @@
 
     block = pl.ds(TOP, 8)
     loads = [
-        pltpu.make_async_copy(v_hbm, VP.at[pl.ds(0, 3), pl.ds(2, 8), block], load_sem.at[0]),
-        pltpu.make_async_copy(d_hbm, VP.at[pl.ds(3, 3), pl.ds(2, 8), block], load_sem.at[1]),
-        pltpu.make_async_copy(p_hbm, PP.at[pl.ds(1, 8), block], load_sem.at[2]),
-        pltpu.make_async_copy(ph_hbm, HP.at[pl.ds(1, 8)], load_sem.at[3]),
-        pltpu.make_async_copy(b_hbm, BF, load_sem.at[4]),
-        pltpu.make_async_copy(fac_hbm, fac_ref, load_sem.at[5]),
-        pltpu.make_async_copy(exp_hbm, exp_ref, load_sem.at[6]),
-        pltpu.make_async_copy(yld_hbm, yld_ref, load_sem.at[7]),
+        pltpu.make_async_copy(v_hbm, VP.at[pl.ds(0, 3), pl.ds(2, 8), block], send_sem.at[0]),
+        pltpu.make_async_copy(d_hbm, VP.at[pl.ds(3, 3), pl.ds(2, 8), block], send_sem.at[1]),
+        pltpu.make_async_copy(p_hbm, PP.at[pl.ds(1, 8), block], send_sem.at[2]),
+        pltpu.make_async_copy(ph_hbm, HP.at[pl.ds(1, 8)], send_sem.at[3]),
+        pltpu.make_async_copy(b_hbm, BF, load_sem.at[0]),
+        pltpu.make_async_copy(fac_hbm, fac_ref, load_sem.at[1]),
+        pltpu.make_async_copy(exp_hbm, exp_ref, load_sem.at[2]),
+        pltpu.make_async_copy(yld_hbm, yld_ref, load_sem.at[3]),
     ]
     for load in loads:
         load.start()
@@ -68,44 +82,48 @@
     for ref in (YR, ZR, XZ, YZ, ER):
         ref[...] = jnp.zeros(ref.shape, f32)
 
-    counter = [0]
-
-    def message(step, pairs):
+    senders, counter = {}, [0]
+
+    def remote(src, dst, i, j, target):
+        return pltpu.make_async_remote_copy(
+            src_ref=src, dst_ref=dst, send_sem=send_sem.at[i], recv_sem=recv_sem.at[j],
+            device_id=target, device_id_type=MESH,
+        )
+
+    def message(step, pairs, whole=None):
         send = functools.reduce(jnp.logical_and, [has[a, s] for a, s in step.items()])
         recv = functools.reduce(jnp.logical_and, [has[a, -s] for a, s in step.items()])
         target = {a: me[a] + s for a, s in step.items()}
-        copies = []
-        for src, dst in pairs:
-            i = counter[0]
-            counter[0] += 1
-            copies.append(
-                pltpu.make_async_remote_copy(
-                    src_ref=src, dst_ref=dst, send_sem=send_sem.at[i], recv_sem=recv_sem.at[i],
-                    device_id=target, device_id_type=MESH,
-                )
-            )
-        return send, recv, copies
+        i = senders.setdefault(tuple(step.items()), len(senders))
+        j = counter[0]
+        counter[0] += 1
+        copies = [remote(src, dst, i, j, target) for src, dst in pairs]
+        return send, recv, copies, remote(whole, whole, i, j, target) if whole is not None else copies[0]
 
     def start(messages):
-        for send, _, copies in messages:
+        for send, _, copies, _ in messages:
             @pl.when(send)
             def _():
                 for copy in copies:
                     copy.start()
 
     def arrived(messages):
-        for _, recv, copies in messages:
+        for _, recv, _, wait in messages:
             @pl.when(recv)
             def _():
-                for copy in copies:
-                    copy.wait_recv()
-
-    def sent(messages):
-        for send, _, copies in messages:
+                wait.wait_recv()
+
+    def sent():
+        for step, i in senders.items():
+            size = {1: YS.at[0] if step[0][0] != "gz" else WS.at[pl.ds(0, 2)]}.get(len(step))
+            if size is None:
+                names = {step[0][0], step[1][0]}
+                size = WS.at[pl.ds(0, 2)] if names == {"gy", "gz"} else WS.at[pl.ds(0, 1)]
+            send = functools.reduce(jnp.logical_and, [has[a, s] for a, s in step])
+
             @pl.when(send)
             def _():
-                for copy in copies:
-                    copy.wait_send()
+                remote(size, size, i, 0, {a: me[a] + s for a, s in step}).wait_send()
 
     both = (1, -1)
     hi = lambda s: (s + 1) // 2
@@ -118,11 +136,11 @@
         x_near.append(message({"gx": s}, [
             (VP.at[:, near_from, block], VP.at[:, near_to, block]),
             (PP.at[p_from, block], PP.at[p_to, block]),
-        ]))
+        ], YR.at[lo(s), pl.ds(0, 7)]))
         x_far.append(message({"gx": s}, [
             (VP.at[:, far_from, block], VP.at[:, far_to, block]),
             (HP.at[p_from], HP.at[p_to]),
-        ]))
+        ], YR.at[lo(s), pl.ds(7, 7)]))
         y_near.append(message({"gy": s}, [(YS.at[hi(s), pl.ds(0, 7)], YR.at[lo(s), pl.ds(0, 7)])]))
         y_far.append(message({"gy": s}, [(YS.at[hi(s), pl.ds(7, 7)], YR.at[lo(s), pl.ds(7, 7)])]))
         z_face.append(message({"gz": s}, [(WS.at[pl.ds(0, 2)], ZR.at[lo(s)])]))
@@ -133,15 +151,22 @@
 
     barrier = pltpu.get_barrier_semaphore()
 
-    greeted = {a: reach(n[a], FAR[a]) for a in n}
+    greeted = {"gz": reach(n["gz"], 2), "gy": reach(n["gy"], 2)}
 
     def signal(sem, a, k):
         pl.semaphore_signal(sem, inc=1, device_id={a: lax.rem(me[a] + k, n[a])}, device_id_type=MESH)
 
-    for a in n:
-        for k in greeted[a]:
-            if k in (1, n[a] - 1):
-                signal(barrier, a, k)
+    def signal_x(sem, step):
+        for s in (step, -step):
+            there = jnp.logical_and(me["gx"] + s >= 0, me["gx"] + s < n["gx"])
+
+            @pl.when(there)
+            def _():
+                pl.semaphore_signal(sem, inc=1, device_id={"gx": me["gx"] + s}, device_id_type=MESH)
+
+    def count_x(step):
+        return (me["gx"] + step < n["gx"]).astype(jnp.int32) + (me["gx"] - step >= 0).astype(jnp.int32)
+
     for a, b in (("gx", "gy"), ("gx", "gz"), ("gy", "gz")):
         for s in both:
             for t in both:
@@ -150,27 +175,44 @@
                     pl.semaphore_signal(
                         barrier, inc=1, device_id={a: me[a] + s, b: me[b] + t}, device_id_type=MESH
                     )
-    for a in n:
+    for a in greeted:
         for k in greeted[a]:
-            if k not in (1, n[a] - 1):
-                signal(barrier, a, k)
+            signal(barrier, a, k)
+    signal_x(barrier, 1)
     sides = {a: has[a, 1].astype(jnp.int32) + has[a, -1].astype(jnp.int32) for a in n}
     edges = sides["gx"] * sides["gy"] + sides["gx"] * sides["gz"] + sides["gy"] * sides["gz"]
 
-    ends = [(a, k) for a in ("gz", "gx") for k in greeted[a] if len(greeted[a]) < n[a] - 1 and min(k, n[a] - k) == FAR[a]]
-    lines = [("gy", k) for k in greeted["gy"]]
+    z_rounds = doubling(2, n["gz"] // 2)
+    x_rounds = doubling(1, n["gx"])
+
+    def tell_z(r):
+        if r < len(z_rounds):
+            for k in (z_rounds[r], n["gz"] - z_rounds[r]):
+                signal(know_sem.at[0, r], "gz", k)
+
+    def told_z(r):
+        if r < len(z_rounds):
+            pl.semaphore_wait(know_sem.at[0, r], 2)
+
+    def tell_x(r):
+        if r < len(x_rounds):
+            signal_x(know_sem.at[1, r], x_rounds[r])
+
+    def told_x(r):
+        if r < len(x_rounds):
+            pl.semaphore_wait(know_sem.at[1, r], count_x(x_rounds[r]))
 
     for load in loads[:4]:
         load.wait()
 
     def y_layer(c, y):
-        return VP[c, pl.ds(2, 8), TOP + y]
+        return take_rows(VP.at[c], 2, TOP + y)
 
     for side, near, far in ((0, 0, 1), (1, 7, 6)):
         for c in range(6):
             YS[side, c] = y_layer(c, near)
             YS[side, 8 + c] = y_layer(c, far)
-        YS[side, 6] = PP[pl.ds(1, 8), TOP + near]
+        YS[side, 6] = take_rows(PP, 1, TOP + near)
         YS[side, 7] = HP[pl.ds(1, 8), near, :].astype(f32)
         for s, xp in ((0, 2), (1, 9)):
             for c in range(6):
@@ -205,11 +247,11 @@
             near_zy = jnp.where(pair == k, roll(YS[side, c], 2 * k + 1, 1), near_zy)
     WS[2] = near_zy
 
-    pl.semaphore_wait(barrier, sum(len(ks) for ks in greeted.values()) + edges)
-    for group in (x_near, y_near, z_face, xy_edge, xz_edge, yz_edge, x_far, y_far):
+    pl.semaphore_wait(barrier, sum(len(ks) for ks in greeted.values()) + sides["gx"] + edges)
+    for group in (z_face, x_near, xz_edge, y_near, xy_edge, yz_edge, x_far, y_far):
         start(group)
-    for a, k in ends:
-        signal(know_sem.at[0], a, k)
+    tell_z(0)
+    tell_x(0)
 
     for load in loads[5:]:
         load.wait()
@@ -234,6 +276,10 @@
             out = tuple(jnp.where(hit, mine, other) for mine, other in zip(table[k], out))
         return out
 
+    for x in range(8):
+        for i, value in enumerate(params(HP[x + 1])):
+            PR[i, x] = value
+
     def tensor(g):
         return (
             g[0][0], g[1][1], g[2][2],
@@ -250,13 +296,13 @@
         total = creep + plastic
         return inverse, creep, plastic, total, creep * plastic / total
 
-    def stresses(g, ids, wanted, mask=None):
-        factor, power, half_yield = params(ids)
+    def stresses(g, material, wanted, mask=None):
+        factor, power, half_yield = material
         base, change = tensor(g[:3]), tensor(g[3:])
         inverse, creep, plastic, total, harmonic = flow(0.125 * dot(base, base) + 0.01, factor, power, half_yield)
-        viscosity = harmonic + 0.05
+        viscosity = 0.5 * harmonic + 0.025
         slope = harmonic * (inverse * inverse) * (plastic * power - 0.5 * creep) / total
-        along = slope * (0.25 * dot(base, change))
+        along = slope * (0.125 * dot(base, change))
         if mask is not None:
             viscosity, along = viscosity * mask, along * mask
         fields = [
@@ -265,7 +311,7 @@
         ]
         for a in LENGTHS:
             trial = tuple(e + f if a == 1.0 else e + a * f for e, f in zip(base, change))
-            viscosity = flow(0.125 * dot(trial, trial) + 0.01, factor, power, half_yield)[4] + 0.05
+            viscosity = 0.5 * flow(0.125 * dot(trial, trial) + 0.01, factor, power, half_yield)[4] + 0.025
             if mask is not None:
                 viscosity = viscosity * mask
             fields.append({c: viscosity * trial[c] for c in wanted})
@@ -275,7 +321,7 @@
         return jnp.where(last_lane, ends, roll(plane, -1, 1)) - jnp.where(first_lane, ends, roll(plane, 1, 1))
 
     def ends_of(packed, k):
-        return roll(packed, -(2 * k + 1), 1)
+        return pltpu.roll(packed, 127 - 2 * k, 1)
 
     def joined(below, above):
         return jnp.where(odd, roll(below, 1, 1), roll(above, -1, 1))
@@ -301,33 +347,51 @@
             for c, value in field.items():
                 SS[f, c, xs, block] = value
 
+    told_z(0)
+    tell_z(1)
+    told_x(0)
+    tell_x(1)
     arrived(z_face)
     arrived(y_near)
     near_halo = joined(ZR[0, 1], ZR[1, 1])
     far_halo = jnp.where(odd, roll(ZR[0, 0], 2, 1), roll(ZR[1, 0], -2, 1))
     for side, row in ((0, TOP - 1), (1, TOP + 8)):
         for c in range(6):
-            VP[c, pl.ds(2, 8), row] = YR[side, c]
-        PP[pl.ds(1, 8), row] = YR[side, 6]
-    for x in range(1, 7):
-        store_plane(x + 1, stresses(plane_differences(x + 2, near_halo, x), HP[x + 1], every))
+            put_rows(VP.at[c], 2, row, YR[side, c])
+        put_rows(PP, 1, row, YR[side, 6])
+
+    def own_plane(x):
+        material = tuple(PR[i, x] for i in range(3))
+        store_plane(x + 1, stresses(plane_differences(x + 2, near_halo, x), material, every))
+
+    def some_planes(i, carry):
+        for k in range(TOGETHER):
+            own_plane(1 + TOGETHER * i + k)
+        return carry
+
+    lax.fori_loop(0, 6 // TOGETHER, some_planes, 0)
 
     arrived(x_near)
-    for x in (0, 7):
-        store_plane(x + 1, stresses(plane_differences(x + 2, near_halo, x), HP[x + 1], every))
+    own_plane(0)
+    own_plane(7)
+    arrived(xz_edge)
+    arrived(yz_edge)
+    x_ends = [joined(XZ[side, 0, 0], XZ[side, 1, 0]) for side in range(2)]
+    inner = WS[1]
+    y_ends = [joined(YZ[side, 0, 0], YZ[side, 1, 0]) for side in range(2)]
+    column = pair & 7
+    out_z = jnp.where(odd, inner - far_halo, far_halo - inner)
+    out_y = roll(jnp.where(sub == 0, y_ends[1], near_halo), -1, 0) - roll(
+        jnp.where(sub == 7, y_ends[0], near_halo), 1, 0
+    )
+    out_x = jnp.where(column == 7, roll(x_ends[1], 14, 1), roll(near_halo, -2, 1)) - jnp.where(
+        column == 0, roll(x_ends[0], -14, 1), roll(near_halo, 2, 1)
+    )
+    g = [tuple(roll(o, -16 * c, 1) if c else o for o in (out_x, out_y, out_z)) for c in range(6)]
+    mask = jnp.where(odd, flag("gz", -1), flag("gz", 1))
+    z_fields = stresses(g, params(roll(near_halo, -112, 1)), ALONG[2], mask)
+
     arrived(xy_edge)
-    arrived(xz_edge)
-    x_ends = [joined(XZ[side, 0, 0], XZ[side, 1, 0]) for side in range(2)]
-    for s, xp in ((0, 1), (1, 10)):
-        for t, row in ((0, TOP - 1), (1, TOP + 8)):
-            for c in range(6):
-                VP[c, xp, pl.ds(row, 1)] = ER[s, t, pl.ds(c, 1)]
-    arrived(x_far)
-    for side, xp, x in ((0, 1, 7), (1, 10, 0)):
-        g = plane_differences(xp, x_ends[side], x)
-        store_plane(xp - 1, stresses(g, HP[xp - 1], ALONG[0], flag("gx", 2 * side - 1)))
-
-    arrived(yz_edge)
     arrived(y_far)
     for side in range(2):
         packed = joined(YZ[side, 0, 1], YZ[side, 1, 1])
@@ -342,30 +406,26 @@
                 outward if side == 0 else -outward,
                 across_z(centre, ends_of(packed, 8 * (1 - side) + c)),
             ))
-        fields = stresses(g, YR[side, 7], ALONG[1], flag("gy", 2 * side - 1))
+        fields = stresses(g, params(YR[side, 7]), ALONG[1], flag("gy", 2 * side - 1))
         row = TOP - 1 if side == 0 else TOP + 8
         for f, field in enumerate(fields):
             for c, value in field.items():
-                SS[f, c, pl.ds(1, 8), row] = value
-
-    inner = WS[1]
-    y_ends = [joined(YZ[side, 0, 0], YZ[side, 1, 0]) for side in range(2)]
-    column = pair & 7
-    out_z = jnp.where(odd, inner - far_halo, far_halo - inner)
-    out_y = roll(jnp.where(sub == 0, y_ends[1], near_halo), -1, 0) - roll(
-        jnp.where(sub == 7, y_ends[0], near_halo), 1, 0
-    )
-    out_x = jnp.where(column == 7, roll(x_ends[1], 14, 1), roll(near_halo, -2, 1)) - jnp.where(
-        column == 0, roll(x_ends[0], -14, 1), roll(near_halo, 2, 1)
-    )
-    g = [tuple(roll(o, -16 * c, 1) if c else o for o in (out_x, out_y, out_z)) for c in range(6)]
-    mask = jnp.where(odd, flag("gz", -1), flag("gz", 1))
-    z_fields = stresses(g, roll(near_halo, -112, 1), ALONG[2], mask)
-
-    if ends:
-        pl.semaphore_wait(know_sem.at[0], len(ends))
-    for a, k in lines:
-        signal(know_sem.at[1], a, k)
+                put_rows(SS.at[f, c], 1, row, value)
+
+    for s, xp in ((0, 1), (1, 10)):
+        for t, row in ((0, TOP - 1), (1, TOP + 8)):
+            for c in range(6):
+                VP[c, xp, pl.ds(row, 1)] = ER[s, t, pl.ds(c, 1)]
+    arrived(x_far)
+    for side, xp, x in ((0, 1, 7), (1, 10, 0)):
+        g = plane_differences(xp, x_ends[side], x)
+        store_plane(xp - 1, stresses(g, params(HP[xp - 1]), ALONG[0], flag("gx", 2 * side - 1)))
+
+    for r in range(1, len(z_rounds)):
+        told_z(r)
+        tell_z(r + 1)
+    told_x(1)
+    tell_x(2)
 
     loads[4].wait()
     sums = [zero] * 8
@@ -385,7 +445,7 @@
                 change = SS[f, cx, xs + 1, block] - SS[f, cx, xs - 1, block]
                 change = change + (SS[f, cy, xs, pl.ds(TOP + 1, 8)] - SS[f, cy, xs, pl.ds(TOP - 1, 8)])
                 change = change + across_z(SS[f, cz, xs, block], ends_of(z_fields[f][cz], x))
-                out.append(0.5 * change if f == 1 else 0.5 * change + loading)
+                out.append(change if f == 1 else change + loading)
             chosen = out[5]
             for k in (2, 1, 0):
                 chosen = jnp.where(picked == k, out[2 + k], chosen)
@@ -400,8 +460,7 @@
         stacked = jnp.where(sub == k, jnp.sum(sums[k], axis=0, keepdims=True), stacked)
     totals = jnp.sum(stacked, axis=1, keepdims=True)
     row = jnp.sum(jnp.where(lane == sub, totals, 0.0), axis=0, keepdims=True)
-    shares = []
-    for axes, ref, sems in ((("gz",), RZ, rz_sem), (("gx", "gy"), RP, rp_sem)):
+    for stage, (axes, ref) in enumerate(((("gz",), RZ), (("gx", "gy"), RP))):
         offsets = [()]
         for a in axes:
             offsets = [o + (k,) for o in offsets for k in range(n[a])]
@@ -409,38 +468,35 @@
         mine = 0
         for a in axes:
             mine = mine * n[a] + me[a]
+        if len(axes) == 2:
+            for r in range(2, len(x_rounds)):
+                told_x(r)
+                tell_x(r + 1)
         ref[mine] = row
-        if len(axes) == 2:
-            pl.semaphore_wait(know_sem.at[1], len(lines))
-        copies = []
-        for i, o in sorted(enumerate(offsets), key=lambda item: -hops(item[1])):
-            if any(o):
-                copies.append(
-                    pltpu.make_async_remote_copy(
-                        src_ref=ref.at[mine], dst_ref=ref.at[mine],
-                        send_sem=sems.at[0, i], recv_sem=sems.at[1, i],
-                        device_id={a: lax.rem(me[a] + k, n[a]) for k, a in zip(o, axes)},
-                        device_id_type=MESH,
-                    )
-                )
-        for copy in copies:
-            copy.start()
-        for copy in copies:
-            copy.wait_recv()
+
+        def share(rows, target):
+            return pltpu.make_async_remote_copy(
+                src_ref=rows, dst_ref=rows, send_sem=load_sem.at[stage], recv_sem=sum_sem.at[stage],
+                device_id=target, device_id_type=MESH,
+            )
+
+        others = sorted((o for o in offsets if any(o)), key=lambda o: -hops(o))
+        targets = [{a: lax.rem(me[a] + k, n[a]) for k, a in zip(o, axes)} for o in others]
+        for target in targets:
+            share(ref.at[mine], target).start()
+        if stage == 0:
+            sent()
+        whole = share(ref.at[pl.ds(0, len(others))], targets[0])
+        whole.wait_send()
+        whole.wait_recv()
         rows = [ref[k] for k in range(len(offsets))]
         while len(rows) > 1:
             rows = [sum(rows[k:k + 2]) for k in range(0, len(rows), 2)]
         row = rows[0]
-        shares += copies
     cells = 3.0 * (8 * n["gx"]) * (8 * n["gy"]) * (128 * n["gz"])
     norms = jnp.sqrt(row / cells + 1e-6)
     norms_ref[pl.ds(0, 1)] = norms[:, 0:4]
     norms_ref[pl.ds(1, 1)] = roll(jnp.broadcast_to(norms, (8, 128)), -4, 1)[0:1, 0:4]
-
-    for copy in shares:
-        copy.wait_send()
-    for group in (x_near, y_near, z_face, xy_edge, xz_edge, yz_edge, x_far, y_far):
-        sent(group)
 
 
 def write_out(*refs):
@@ -483,14 +539,14 @@
                 pltpu.VMEM((2, 2, 8, 128), f32),
                 pltpu.VMEM((2, 2, 8, 128), f32),
                 pltpu.VMEM((6, 6, 10, ROWS, 128), f32),
+                pltpu.VMEM((3, 8, 8, 128), f32),
                 pltpu.VMEM((sizes[2], 1, 128), f32),
                 pltpu.VMEM((sizes[0] * sizes[1], 1, 128), f32),
-                pltpu.SemaphoreType.DMA((8,)),
-                pltpu.SemaphoreType.DMA((26,)),
-                pltpu.SemaphoreType.DMA((26,)),
-                pltpu.SemaphoreType.DMA((2, sizes[2])),
-                pltpu.SemaphoreType.DMA((2, sizes[0] * sizes[1])),
-                pltpu.SemaphoreType.REGULAR((2,)),
+                pltpu.SemaphoreType.DMA((4,)),
+                pltpu.SemaphoreType.DMA((18,)),
+                pltpu.SemaphoreType.DMA((22,)),
+                pltpu.SemaphoreType.DMA((2,)),
+                pltpu.SemaphoreType.REGULAR((2, 3)),
             ],
             compiler_params=pltpu.CompilerParams(
                 collective_id=0, has_side_effects=True, vmem_limit_bytes=16 * 1024 * 1024

time: 33.1 us -> 31.6 us (0.955)
  Pallas kernels: 31.7 us -> 30.2 us
    pallas_call x1, Pallas kernels: 31 us -> 29.5 us  [body(): pl.pallas_call(functools.partial(kernel, sizes), out_shape=outputs, in_sp...]
where the time goes in v5:
time: 31.6 us; the launch traced here: 31.5 us
  Pallas kernels  30.2 us (96%)
  between operations  1.29 us (4%)
    pallas_call x1, Pallas kernels, body(): pl.pallas_call(functools.partial(kernel, sizes), out_shape=outputs, in_sp...  29.5 us
    pallas_call x1, Pallas kernels, body(): pl.pallas_call(write_out, out_shape=outputs, in_specs=[inside] * 3, out_s...  0.71 us

profile of v5, /device:TPU:1, one launch (start us, length us, event | category | flops | bytes accessed | tf_op | source)
XLA Modules:
  0.0 31.5 jit_solution(448573994926410166)
XLA Ops:
  1.3 29.5 %line_search.1 = (f32[2,4]{1,0:T(2,128)S(1)}, f32[3,8,8,128]{3,2,1,0:T(8,128)S(1)}, f32[3,8,8,128]{3,2,1,0:T(8,128)S(1)}) custom-call(f32[3,8,8,128]{3,2,1,0:T(8,128)} %v_hbm.1, f32[3,8,8,128]{3,2,1,0:T(8,128)} %d_hbm.1, f32[8,8,128]{2,1,0:T(8,128)} %p_hbm.1, f32[3,8,8,128]{3,2,1,0:T(8,128)} %b_hbm.1, s32[8,8,128]{2,1,0:T(8,128)} %ph_hbm.1, f32[4]{0:T(128)} %fac_hbm.1, ...), custom_call_target="tpu_custom_call" | custom-call | tf_op jit(solution)/shard_map/line_search/pallas_call | solution.py:520
  30.8 0.7 %write_out.1 = (f32[2,4]{1,0:T(2,128)}, f32[3,8,8,128]{3,2,1,0:T(8,128)}, f32[3,8,8,128]{3,2,1,0:T(8,128)}) custom-call(f32[2,4]{1,0:T(2,128)S(1)} %get-tuple-element.6.refs_0_, f32[3,8,8,128]{3,2,1,0:T(8,128)S(1)} %get-tuple-element.7.refs_1_, f32[3,8,8,128]{3,2,1,0:T(8,128)S(1)} %get-tuple-element.8.refs_2_), custom_call_target="tpu_custom_call" | custom-call | tf_op jit(solution)/shard_map/write_out/pallas_call | solution.py:556

commit v6 on v5

--- a/solution.py
+++ b/solution.py
@@ -82,72 +82,75 @@
     for ref in (YR, ZR, XZ, YZ, ER):
         ref[...] = jnp.zeros(ref.shape, f32)
 
-    senders, counter = {}, [0]
-
-    def remote(src, dst, i, j, target):
+    groups = []
+
+    def group(size):
+        groups.append((len(groups), size, []))
+        return groups[-1]
+
+    def remote(src, dst, g, step):
         return pltpu.make_async_remote_copy(
-            src_ref=src, dst_ref=dst, send_sem=send_sem.at[i], recv_sem=recv_sem.at[j],
-            device_id=target, device_id_type=MESH,
+            src_ref=src, dst_ref=dst, send_sem=send_sem.at[g], recv_sem=recv_sem.at[g],
+            device_id={a: me[a] + s for a, s in step.items()}, device_id_type=MESH,
         )
 
-    def message(step, pairs, whole=None):
+    def message(into, step, pairs):
         send = functools.reduce(jnp.logical_and, [has[a, s] for a, s in step.items()])
         recv = functools.reduce(jnp.logical_and, [has[a, -s] for a, s in step.items()])
-        target = {a: me[a] + s for a, s in step.items()}
-        i = senders.setdefault(tuple(step.items()), len(senders))
-        j = counter[0]
-        counter[0] += 1
-        copies = [remote(src, dst, i, j, target) for src, dst in pairs]
-        return send, recv, copies, remote(whole, whole, i, j, target) if whole is not None else copies[0]
-
-    def start(messages):
-        for send, _, copies, _ in messages:
+        into[2].append((send, recv, step, [remote(src, dst, into[0], step) for src, dst in pairs]))
+
+    def start(into):
+        for send, _, _, copies in into[2]:
             @pl.when(send)
             def _():
                 for copy in copies:
                     copy.start()
 
-    def arrived(messages):
-        for _, recv, _, wait in messages:
-            @pl.when(recv)
-            def _():
-                wait.wait_recv()
+    def wait_all(into, which):
+        g, size, messages = into
+        count = sum(m[which].astype(jnp.int32) for m in messages)
+        for k in (1, 2, 4):
+            if k <= len(messages):
+                @pl.when(count == k)
+                def _():
+                    some = YS.at[0, pl.ds(0, k * size)]
+                    whole = remote(some, some, g, messages[0][2])
+                    if which:
+                        whole.wait_recv()
+                    else:
+                        whole.wait_send()
+
+    def arrived(into):
+        wait_all(into, 1)
 
     def sent():
-        for step, i in senders.items():
-            size = {1: YS.at[0] if step[0][0] != "gz" else WS.at[pl.ds(0, 2)]}.get(len(step))
-            if size is None:
-                names = {step[0][0], step[1][0]}
-                size = WS.at[pl.ds(0, 2)] if names == {"gy", "gz"} else WS.at[pl.ds(0, 1)]
-            send = functools.reduce(jnp.logical_and, [has[a, s] for a, s in step])
-
-            @pl.when(send)
-            def _():
-                remote(size, size, i, 0, {a: me[a] + s for a, s in step}).wait_send()
+        for into in groups:
+            wait_all(into, 0)
 
     both = (1, -1)
     hi = lambda s: (s + 1) // 2
     lo = lambda s: (1 - s) // 2
-    x_near, x_far, y_near, y_far, z_face, xz_edge, yz_edge, xy_edge = ([] for _ in range(8))
+    x_near, x_far, y_near, y_far = (group(7) for _ in range(4))
+    z_face, xz_edge, yz_edge, xy_edge = group(2), group(1), group(2), group(1)
     for s in both:
         near_from, near_to = (9, 1) if s == 1 else (2, 10)
         far_from, far_to = (8, 0) if s == 1 else (3, 11)
         p_from, p_to = (8, 0) if s == 1 else (1, 9)
-        x_near.append(message({"gx": s}, [
+        message(x_near, {"gx": s}, [
             (VP.at[:, near_from, block], VP.at[:, near_to, block]),
             (PP.at[p_from, block], PP.at[p_to, block]),
-        ], YR.at[lo(s), pl.ds(0, 7)]))
-        x_far.append(message({"gx": s}, [
+        ])
+        message(x_far, {"gx": s}, [
             (VP.at[:, far_from, block], VP.at[:, far_to, block]),
             (HP.at[p_from], HP.at[p_to]),
-        ], YR.at[lo(s), pl.ds(7, 7)]))
-        y_near.append(message({"gy": s}, [(YS.at[hi(s), pl.ds(0, 7)], YR.at[lo(s), pl.ds(0, 7)])]))
-        y_far.append(message({"gy": s}, [(YS.at[hi(s), pl.ds(7, 7)], YR.at[lo(s), pl.ds(7, 7)])]))
-        z_face.append(message({"gz": s}, [(WS.at[pl.ds(0, 2)], ZR.at[lo(s)])]))
+        ])
+        message(y_near, {"gy": s}, [(YS.at[hi(s), pl.ds(0, 7)], YR.at[lo(s), pl.ds(0, 7)])])
+        message(y_far, {"gy": s}, [(YS.at[hi(s), pl.ds(7, 7)], YR.at[lo(s), pl.ds(7, 7)])])
+        message(z_face, {"gz": s}, [(WS.at[pl.ds(0, 2)], ZR.at[lo(s)])])
         for t in both:
-            xz_edge.append(message({"gx": s, "gz": t}, [(WS.at[pl.ds(1, 1)], XZ.at[lo(s), lo(t)])]))
-            yz_edge.append(message({"gy": s, "gz": t}, [(WS.at[pl.ds(1, 2)], YZ.at[lo(s), lo(t)])]))
-            xy_edge.append(message({"gx": s, "gy": t}, [(ES.at[hi(s), hi(t)], ER.at[lo(s), lo(t)])]))
+            message(xz_edge, {"gx": s, "gz": t}, [(WS.at[pl.ds(1, 1)], XZ.at[lo(s), lo(t)])])
+            message(yz_edge, {"gy": s, "gz": t}, [(WS.at[pl.ds(1, 2)], YZ.at[lo(s), lo(t)])])
+            message(xy_edge, {"gx": s, "gy": t}, [(ES.at[hi(s), hi(t)], ER.at[lo(s), lo(t)])])
 
     barrier = pltpu.get_barrier_semaphore()
 
@@ -248,8 +251,8 @@
     WS[2] = near_zy
 
     pl.semaphore_wait(barrier, sum(len(ks) for ks in greeted.values()) + sides["gx"] + edges)
-    for group in (z_face, x_near, xz_edge, y_near, xy_edge, yz_edge, x_far, y_far):
-        start(group)
+    for into in (z_face, xz_edge, yz_edge, xy_edge, x_near, y_near, x_far, y_far):
+        start(into)
     tell_z(0)
     tell_x(0)
 
@@ -543,8 +546,8 @@
                 pltpu.VMEM((sizes[2], 1, 128), f32),
                 pltpu.VMEM((sizes[0] * sizes[1], 1, 128), f32),
                 pltpu.SemaphoreType.DMA((4,)),
-                pltpu.SemaphoreType.DMA((18,)),
-                pltpu.SemaphoreType.DMA((22,)),
+                pltpu.SemaphoreType.DMA((8,)),
+                pltpu.SemaphoreType.DMA((8,)),
                 pltpu.SemaphoreType.DMA((2,)),
                 pltpu.SemaphoreType.REGULAR((2, 3)),
             ],

time: 31.6 us -> 31.4 us (level)
  no operation moved by 1% of the time
where the time goes in v6:
time: 31.4 us; the launch traced here: 31.3 us
  Pallas kernels  30 us (96%)
  between operations  1.29 us (4%)
    pallas_call x1, Pallas kernels, body(): pl.pallas_call(functools.partial(kernel, sizes), out_shape=outputs, in_sp...  29.3 us
    pallas_call x1, Pallas kernels, body(): pl.pallas_call(write_out, out_shape=outputs, in_specs=[inside] * 3, out_s...  0.71 us

profile of v6, /device:TPU:1, one launch (start us, length us, event | category | flops | bytes accessed | tf_op | source)
XLA Modules:
  0.0 31.3 jit_solution(14459620154548030316)
XLA Ops:
  1.3 29.3 %line_search.1 = (f32[2,4]{1,0:T(2,128)S(1)}, f32[3,8,8,128]{3,2,1,0:T(8,128)S(1)}, f32[3,8,8,128]{3,2,1,0:T(8,128)S(1)}) custom-call(f32[3,8,8,128]{3,2,1,0:T(8,128)} %v_hbm.1, f32[3,8,8,128]{3,2,1,0:T(8,128)} %d_hbm.1, f32[8,8,128]{2,1,0:T(8,128)} %p_hbm.1, f32[3,8,8,128]{3,2,1,0:T(8,128)} %b_hbm.1, s32[8,8,128]{2,1,0:T(8,128)} %ph_hbm.1, f32[4]{0:T(128)} %fac_hbm.1, ...), custom_call_target="tpu_custom_call" | custom-call | tf_op jit(solution)/shard_map/line_search/pallas_call | solution.py:523
  30.6 0.7 %write_out.1 = (f32[2,4]{1,0:T(2,128)}, f32[3,8,8,128]{3,2,1,0:T(8,128)}, f32[3,8,8,128]{3,2,1,0:T(8,128)}) custom-call(f32[2,4]{1,0:T(2,128)S(1)} %get-tuple-element.6.refs_0_, f32[3,8,8,128]{3,2,1,0:T(8,128)S(1)} %get-tuple-element.7.refs_1_, f32[3,8,8,128]{3,2,1,0:T(8,128)S(1)} %get-tuple-element.8.refs_2_), custom_call_target="tpu_custom_call" | custom-call | tf_op jit(solution)/shard_map/write_out/pallas_call | solution.py:559

commit v7 on v6

--- a/solution.py
+++ b/solution.py
@@ -350,10 +350,6 @@
             for c, value in field.items():
                 SS[f, c, xs, block] = value
 
-    told_z(0)
-    tell_z(1)
-    told_x(0)
-    tell_x(1)
     arrived(z_face)
     arrived(y_near)
     near_halo = joined(ZR[0, 1], ZR[1, 1])
@@ -373,6 +369,10 @@
         return carry
 
     lax.fori_loop(0, 6 // TOGETHER, some_planes, 0)
+    told_z(0)
+    tell_z(1)
+    told_x(0)
+    tell_x(1)
 
     arrived(x_near)
     own_plane(0)

time: 31.4 us -> 32.3 us (1.029)
  Pallas kernels: 30 us -> 30.8 us
    pallas_call x1, Pallas kernels: 29.3 us -> 30.1 us  [body(): pl.pallas_call(functools.partial(kernel, sizes), out_shape=outputs, in_sp...]
where the time goes in v7:
time: 32.3 us; the launch traced here: 32.1 us
  Pallas kernels  30.8 us (95%)
  between operations  1.29 us (4%)
    pallas_call x1, Pallas kernels, body(): pl.pallas_call(functools.partial(kernel, sizes), out_shape=outputs, in_sp...  30.1 us
    pallas_call x1, Pallas kernels, body(): pl.pallas_call(write_out, out_shape=outputs, in_specs=[inside] * 3, out_s...  0.71 us

profile of v7, /device:TPU:1, one launch (start us, length us, event | category | flops | bytes accessed | tf_op | source)
XLA Modules:
  0.0 32.1 jit_solution(4886352618564156670)
XLA Ops:
  1.3 30.1 %line_search.1 = (f32[2,4]{1,0:T(2,128)S(1)}, f32[3,8,8,128]{3,2,1,0:T(8,128)S(1)}, f32[3,8,8,128]{3,2,1,0:T(8,128)S(1)}) custom-call(f32[3,8,8,128]{3,2,1,0:T(8,128)} %v_hbm.1, f32[3,8,8,128]{3,2,1,0:T(8,128)} %d_hbm.1, f32[8,8,128]{2,1,0:T(8,128)} %p_hbm.1, f32[3,8,8,128]{3,2,1,0:T(8,128)} %b_hbm.1, s32[8,8,128]{2,1,0:T(8,128)} %ph_hbm.1, f32[4]{0:T(128)} %fac_hbm.1, ...), custom_call_target="tpu_custom_call" | custom-call | tf_op jit(solution)/shard_map/line_search/pallas_call | solution.py:523
  31.4 0.7 %write_out.1 = (f32[2,4]{1,0:T(2,128)}, f32[3,8,8,128]{3,2,1,0:T(8,128)}, f32[3,8,8,128]{3,2,1,0:T(8,128)}) custom-call(f32[2,4]{1,0:T(2,128)S(1)} %get-tuple-element.6.refs_0_, f32[3,8,8,128]{3,2,1,0:T(8,128)S(1)} %get-tuple-element.7.refs_1_, f32[3,8,8,128]{3,2,1,0:T(8,128)S(1)} %get-tuple-element.8.refs_2_), custom_call_target="tpu_custom_call" | custom-call | tf_op jit(solution)/shard_map/write_out/pallas_call | solution.py:559
